TPU v7x, 256 devices: a whole 4x4x8 slice. The times are simulated.
256 devices in a mesh: section: 4 (over y_hi, core), dp: 64 (over y_lo, x, z).
Axes of the slice: x: 4, y: 4 (y_hi: 2, y_lo: 2; y = y_hi * 2 + y_lo), z: 8, core: 2. Of those that a mesh axis runs over, the one named last changes fastest.
Arguments:
- latents: bfloat16 [128, 4, 128], P('dp'), may hold values from -6 to 6
- noise: bfloat16 [128, 4, 128], P('dp'), may hold values from -6 to 6
- timesteps: int32 [128], P('dp'), may hold values from 0 to 999
- cameras: int32 [128, 4], P('dp'), may hold values from 0 to 31
- embed_in: bfloat16 [4, 1024], replicated, may hold values from -3 to 3
- camera_table: bfloat16 [32, 1024], replicated, may hold values from -6 to 6
- w_mod: bfloat16 [4, 256, 3072], P('section'), may hold values from -0.375 to 0.375
- w_qkv: bfloat16 [4, 1024, 3072], P('section'), may hold values from -0.1875 to 0.1875
- w_out: bfloat16 [4, 1024, 1024], P('section'), may hold values from -0.1875 to 0.1875
- head_out: bfloat16 [4, 1024], replicated, may hold values from -0.1875 to 0.1875
- moment_qkv: float32 [4, 1024, 3072], P('section', 'dp'), may hold values from -6 to 6
- moment_out: float32 [4, 1024, 1024], P('section', 'dp'), may hold values from -6 to 6
- second_qkv: float32 [4, 1024, 3072], P('section', 'dp'), may hold values from 0.25 to 4
- second_out: float32 [4, 1024, 1024], P('section', 'dp'), may hold values from 0.25 to 4
Outputs:
- update_qkv: float32 [4, 1024, 3072], P('section', 'dp')
- update_out: float32 [4, 1024, 1024], P('section', 'dp')
- new_moment_qkv: float32 [4, 1024, 3072], P('section', 'dp')
- new_moment_out: float32 [4, 1024, 1024], P('section', 'dp')
- new_second_qkv: float32 [4, 1024, 3072], P('section', 'dp')
- new_second_out: float32 [4, 1024, 1024], P('section', 'dp')
All inputs are finite; a program needn't handle non-finite values.
Results may differ from a plain program's by a relative error of at most 0.00045.
Values may be sent and summed in bfloat16 or wider, within the bound.
A program may use at most 128 MiB of HBM per device.

v0:
```python
import math

import jax
import jax.numpy as jnp
from jax import lax
from jax.sharding import Mesh
from jax.sharding import PartitionSpec as P

HEADS = 16
HEAD_DIM = 64
SECTION = ("section_0", "section_1")
DP = ("dp_0", "dp_1", "dp_2")
SECTION_DP = ("section_0", "section_1", "dp_0", "dp_1", "dp_2")


def passed_along(x, axis, by):
    devices = lax.axis_size(axis)
    pairs = [(i, i + by) for i in range(devices) if 0 <= i + by < devices]
    return lax.ppermute(x, axis, pairs)


def side_by_side(arrays, axis, dim, along):
    both = jnp.concatenate(arrays, axis=along)
    filled, at, done = (lax.psum_scatter(both, axis, scatter_dimension=dim, tiled=True), 0, [])
    for a in arrays:
        done.append(lax.slice_in_dim(filled, at, at + a.shape[along], axis=along))
        at += a.shape[along]
    return tuple(done)


def over_axes(x, axes):
    for axis in axes:
        x = lax.psum(x, axis)
    return x


def time_embed(step_ids, emb_width):
    half_dim = emb_width // 2
    frequency = jnp.exp(-math.log(10000.0) * jnp.arange(half_dim, dtype=jnp.float32) / half_dim)
    phases = step_ids.astype(jnp.float32)[:, None] * frequency[None, :]
    joined = jnp.concatenate([jnp.cos(phases), jnp.sin(phases)], axis=-1)
    return jax.nn.silu(joined).astype(jnp.bfloat16)


def embed_sample(latent_now, noise_now, step_now, camera_now, embed_in, camera_table):
    step_f = step_now.astype(jnp.float32)
    alpha_bar = jnp.cos((step_f / 1000.0 + 0.008) / 1.008 * (math.pi / 2.0)) ** 2
    noised = jnp.sqrt(alpha_bar) * latent_now.astype(jnp.float32) + jnp.sqrt(
        1.0 - alpha_bar
    ) * noise_now.astype(jnp.float32)
    features = lax.dot_general(
        noised.astype(jnp.bfloat16),
        embed_in,
        (((0,), (0,)), ((), ())),
        preferred_element_type=jnp.float32,
    )
    onehot = (
        camera_now[:, None] == jnp.arange(camera_table.shape[0], dtype=jnp.int32)[None, :]
    ).astype(jnp.bfloat16)
    camera_vec = jnp.dot(onehot, camera_table, preferred_element_type=jnp.float32)
    model_width = embed_in.shape[1]
    views = camera_now.shape[0]
    joined = features.reshape(views, -1, model_width) + camera_vec[:, None, :]
    return joined.reshape(-1, model_width).astype(jnp.bfloat16)


def normed_of(layer_h, shift_mod, scale_mod):
    hidden_f = layer_h.astype(jnp.float32)
    mean_sq = jnp.mean(hidden_f * hidden_f, axis=-1, keepdims=True)
    return (hidden_f * lax.rsqrt(mean_sq + 1e-06) * (1.0 + scale_mod) + shift_mod).astype(
        jnp.bfloat16
    )


def piece_a(layer_h, weight_qkv, shift_mod, scale_mod):
    normed = normed_of(layer_h, shift_mod, scale_mod)
    return jnp.dot(normed, weight_qkv, preferred_element_type=jnp.float32).astype(jnp.bfloat16)


def piece_b(qkv_rows):
    seq_len = qkv_rows.shape[0]
    model_width = qkv_rows.shape[1] // 3
    queries = qkv_rows[:, :model_width].reshape(seq_len, HEADS, HEAD_DIM)
    keys_in = qkv_rows[:, model_width : 2 * model_width].reshape(seq_len, HEADS, HEAD_DIM)
    values_in = qkv_rows[:, 2 * model_width :].reshape(seq_len, HEADS, HEAD_DIM)
    scores = jnp.einsum("qhd,khd->hqk", queries, keys_in, preferred_element_type=jnp.float32) * (
        1.0 / math.sqrt(HEAD_DIM)
    )
    probabilities = jax.nn.softmax(scores, axis=-1).astype(jnp.bfloat16)
    attended = jnp.einsum(
        "hqk,khd->qhd", probabilities, values_in, preferred_element_type=jnp.float32
    )
    return attended.reshape(seq_len, model_width).astype(jnp.bfloat16)


def piece_c(attended, layer_h, weight_out, gate_mod):
    projected = jnp.dot(attended, weight_out, preferred_element_type=jnp.float32)
    return (layer_h.astype(jnp.float32) + gate_mod * projected).astype(jnp.bfloat16)


def output_grad(final_h, head_out, noise_now):

    def squared(hidden_in):
        hidden_f = hidden_in.astype(jnp.float32)
        mean_sq = jnp.mean(hidden_f * hidden_f, axis=-1, keepdims=True)
        normed = (hidden_f * lax.rsqrt(mean_sq + 1e-06)).astype(jnp.bfloat16)
        predicted = lax.dot_general(
            head_out, normed, (((1,), (1,)), ((), ())), preferred_element_type=jnp.float32
        )
        error_val = predicted - noise_now.astype(jnp.float32)
        return jnp.sum(error_val * error_val)

    loss_val, pull_back = jax.vjp(squared, final_h)
    return pull_back(jnp.ones_like(loss_val))[0]


def optimizer_step(gradient, moment, second, factor):
    normalized = gradient * factor
    moment_new = 0.9 * moment + 0.1 * normalized
    second_new = 0.99 * second + 0.01 * normalized * normalized
    return (moment_new / (jnp.sqrt(second_new) + 1e-08), moment_new, second_new)


def pick_row(array, micro_slot):
    return lax.dynamic_index_in_dim(array, micro_slot, 0, keepdims=False)


def put_row(array, value, micro_slot):
    return lax.dynamic_update_index_in_dim(array, value, micro_slot, 0)


def local(
    latents,
    noise,
    timesteps,
    cameras,
    embed_in,
    camera_table,
    w_mod,
    w_qkv,
    w_out,
    head_out,
    moment_qkv,
    moment_out,
    second_qkv,
    second_out,
):
    sections = lax.axis_size(SECTION)
    section_id = lax.axis_index(SECTION)
    last_section = sections - 1
    micro_count = latents.shape[0]
    seq_len = latents.shape[2]
    model_width = w_qkv.shape[1]
    tick_count = micro_count + sections - 1
    w_qkv_layer = w_qkv[0]
    w_out_layer = w_out[0]
    time_emb = time_embed(timesteps, w_mod.shape[1])
    modulation = jnp.dot(time_emb, w_mod[0], preferred_element_type=jnp.float32)
    zero_act = jnp.zeros((seq_len, model_width), jnp.bfloat16)

    def mods_of(micro_slot):
        mod_row = pick_row(modulation, micro_slot)
        return (
            mod_row[:model_width],
            mod_row[model_width : 2 * model_width],
            mod_row[2 * model_width :],
        )

    stored_h = jnp.zeros((micro_count, seq_len, model_width), jnp.bfloat16)
    grad_final = jnp.zeros((micro_count, seq_len, model_width), jnp.bfloat16)
    stored_qkv = None
    stored_attn = None
    buffers = (stored_h, stored_qkv, stored_attn, grad_final)
    sent_act = zero_act
    for tick_num in range(tick_count):
        received = passed_along(sent_act, SECTION, 1) if tick_num > 0 else zero_act
        micro_index = tick_num - section_id
        is_active = (micro_index >= 0) & (micro_index < micro_count)
        micro_slot = jnp.clip(micro_index, 0, micro_count - 1)
        noise_now = pick_row(noise, micro_slot)
        embedded = embed_sample(
            pick_row(latents, micro_slot),
            noise_now,
            pick_row(timesteps, micro_slot),
            pick_row(cameras, micro_slot),
            embed_in,
            camera_table,
        )
        layer_in = jnp.where(section_id == 0, embedded, received)
        shift_mod, scale_mod, gate_mod = mods_of(micro_slot)

        def active(
            state,
            layer_in=layer_in,
            noise_now=noise_now,
            micro_slot=micro_slot,
            shift_mod=shift_mod,
            scale_mod=scale_mod,
            gate_mod=gate_mod,
        ):
            held_h, held_qkv, held_attn, held_grad = state
            qkv_rows = piece_a(layer_in, w_qkv_layer, shift_mod, scale_mod)
            attended = piece_b(qkv_rows)
            layer_out = piece_c(attended, layer_in, w_out_layer, gate_mod)
            head_grad = lax.cond(
                section_id == last_section,
                lambda final_h: output_grad(final_h, head_out, noise_now),
                lambda final_h: jnp.zeros_like(final_h),
                layer_out,
            )
            held_h = put_row(held_h, layer_in, micro_slot)
            held_grad = put_row(held_grad, head_grad, micro_slot)
            return (layer_out, (held_h, held_qkv, held_attn, held_grad))

        def resting(state):
            return (zero_act, state)

        sent_act, buffers = lax.cond(is_active, active, resting, buffers)
    stored_h, stored_qkv, stored_attn, grad_final = buffers
    cot_qkv = jnp.zeros((micro_count, seq_len, 3 * model_width), jnp.bfloat16)
    cot_proj = jnp.zeros((micro_count, seq_len, model_width), jnp.bfloat16)
    back_attn = jnp.zeros((micro_count, seq_len, model_width), jnp.bfloat16)
    back_state = (cot_qkv, cot_proj, back_attn)
    sent_grad = zero_act
    for tick_num in range(tick_count):
        received = passed_along(sent_grad, SECTION, -1) if tick_num > 0 else zero_act
        micro_index = tick_num - (last_section - section_id)
        is_active = (micro_index >= 0) & (micro_index < micro_count)
        micro_slot = jnp.clip(micro_index, 0, micro_count - 1)
        grad_out = jnp.where(section_id == last_section, pick_row(grad_final, micro_slot), received)
        layer_in = pick_row(stored_h, micro_slot)
        shift_mod, scale_mod, gate_mod = mods_of(micro_slot)

        def backward(
            state,
            layer_in=layer_in,
            grad_out=grad_out,
            micro_slot=micro_slot,
            shift_mod=shift_mod,
            scale_mod=scale_mod,
            gate_mod=gate_mod,
        ):
            held_cot_qkv, held_cot_proj, held_attn = state
            qkv_rows = piece_a(layer_in, w_qkv_layer, shift_mod, scale_mod)
            attended = piece_b(qkv_rows)
            held_attn = put_row(held_attn, attended, micro_slot)
            _, pull_c = jax.vjp(
                lambda attn_in, hidden_in: piece_c(attn_in, hidden_in, w_out_layer, gate_mod),
                attended,
                layer_in,
            )
            grad_attn, grad_res = pull_c(grad_out)
            proj_cot = (gate_mod * grad_out.astype(jnp.float32)).astype(jnp.bfloat16)
            _, pull_b = jax.vjp(piece_b, qkv_rows)
            grad_qkv_rows = pull_b(grad_attn)[0]
            _, pull_a = jax.vjp(
                lambda hidden_in: piece_a(hidden_in, w_qkv_layer, shift_mod, scale_mod), layer_in
            )
            grad_hidden = pull_a(grad_qkv_rows)[0]
            grad_total = (grad_hidden.astype(jnp.float32) + grad_res.astype(jnp.float32)).astype(
                jnp.bfloat16
            )
            held_cot_qkv = put_row(held_cot_qkv, grad_qkv_rows, micro_slot)
            held_cot_proj = put_row(held_cot_proj, proj_cot, micro_slot)
            return (grad_total, (held_cot_qkv, held_cot_proj, held_attn))

        def waiting(state):
            return (zero_act, state)

        sent_grad, back_state = lax.cond(is_active, backward, waiting, back_state)
    cot_qkv, cot_proj, back_attn = back_state
    shift_all = modulation[:, None, :model_width]
    scale_all = modulation[:, None, model_width : 2 * model_width]
    rows_all = micro_count * seq_len
    normed_all = normed_of(stored_h, shift_all, scale_all).reshape(rows_all, model_width)
    qkv_shard, out_shard = side_by_side(
        (
            lax.dot_general(
                normed_all,
                cot_qkv.reshape(rows_all, 3 * model_width),
                (((0,), (0,)), ((), ())),
                preferred_element_type=jnp.float32,
            )[None],
            lax.dot_general(
                back_attn.reshape(rows_all, model_width),
                cot_proj.reshape(rows_all, model_width),
                (((0,), (0,)), ((), ())),
                preferred_element_type=jnp.float32,
            )[None],
        ),
        DP,
        1,
        2,
    )
    local_sq = jnp.sum(qkv_shard * qkv_shard) + jnp.sum(out_shard * out_shard)
    total_sq = over_axes(local_sq, SECTION_DP)
    factor = lax.rsqrt(total_sq / (sections * 4 * model_width * model_width) + 1e-12)
    update_qkv, new_moment_qkv, new_second_qkv = optimizer_step(
        qkv_shard, moment_qkv, second_qkv, factor
    )
    update_out, new_moment_out, new_second_out = optimizer_step(
        out_shard, moment_out, second_out, factor
    )
    return (update_qkv, update_out, new_moment_qkv, new_moment_out, new_second_qkv, new_second_out)


def solution(mesh):
    torus = Mesh(
        mesh.devices.reshape(2, 2, 2, 4, 8), ("section_0", "section_1", "dp_0", "dp_1", "dp_2")
    )
    return jax.shard_map(
        local,
        mesh=torus,
        in_specs=(
            P(DP, None, None),
            P(DP, None, None),
            P(DP),
            P(DP, None),
            P(),
            P(),
            P(SECTION, None, None),
            P(SECTION, None, None),
            P(SECTION, None, None),
            P(),
            P(SECTION, DP, None),
            P(SECTION, DP, None),
            P(SECTION, DP, None),
            P(SECTION, DP, None),
        ),
        out_specs=(
            P(SECTION, DP, None),
            P(SECTION, DP, None),
            P(SECTION, DP, None),
            P(SECTION, DP, None),
            P(SECTION, DP, None),
            P(SECTION, DP, None),
        ),
        check_vma=False,
    )
```

profile of v0, /device:TPU:8, one launch (start us, length us, event | category | flops | bytes accessed | tf_op | source)
XLA Modules:
  0.0 638.6 jit_solution(3485924416214371077)
XLA Ops:
  18.8 10.8 %conditional.21 = (bf16[128,1024]{1,0:T(8,128)(2,1)}, bf16[2,128,1024]{2,1,0:T(8,128)(2,1)S(1)}, bf16[2,128,1024]{2,1,0:T(8,128)(2,1)}) conditional(s32[]{:T(128)} %convert_element_type.1107, () %tuple.178, (f32[4,1024]{1,0:T(4,128)S(1)}, f32[4,32,1024]{2,1,0:T(8,128)S(1)}, pred[128,1024]{1,0:T(8,128)(4,1)S(1)}, bf16[128,1024]{1,0:T(8,128)(2,1)S(1)}, ...), branch_computations={%region_0.1_spmd, %region_1.9_spmd} | conditional | flops 1183061632 | bytes 27218128 | solution.py:218
  19.3 4.0 convolution_convert_fusion.1
  25.2 2.8 fusion.18
  32.3 9.6 %conditional.22 = (bf16[128,1024]{1,0:T(8,128)(2,1)}, bf16[2,128,1024]{2,1,0:T(8,128)(2,1)S(1)}, bf16[2,128,1024]{2,1,0:T(8,128)(2,1)}) conditional(s32[]{:T(128)} %convert_element_type.1106, (bf16[2,128,1024]{2,1,0:T(8,128)(2,1)S(1)}, bf16[2,128,1024]{2,1,0:T(8,128)(2,1)}) %tuple.180, (f32[4,1024]{1,0:T(4,128)S(1)}, f32[4,32,1024]{2,1,0:T(8,128)S(1)}, ...), branch_computations={%region_9.10_spmd, %region_10.18_spmd} | conditional | flops 1183061632 | bytes 21975180 | solution.py:218
  32.7 3.8 convolution_convert_fusion.4
  45.5 7.5 %conditional.23 = (bf16[128,1024]{1,0:T(8,128)(2,1)}, bf16[2,128,1024]{2,1,0:T(8,128)(2,1)S(1)}, bf16[2,128,1024]{2,1,0:T(8,128)(2,1)}) conditional(s32[]{:T(128)} %convert_element_type.1105, (bf16[2,128,1024]{2,1,0:T(8,128)(2,1)S(1)}, bf16[2,128,1024]{2,1,0:T(8,128)(2,1)}) %tuple.182, (f32[4,1024]{1,0:T(4,128)S(1)}, ...), branch_computations={%region_18.19_spmd, %region_19.27_spmd} | conditional | flops 1183061632 | bytes 21975180 | solution.py:218
  53.0 7.0 %collective-permute-start.2 = (bf16[128,1024]{1,0:T(8,128)(2,1)}, bf16[128,1024]{1,0:T(8,128)(2,1)S(1)}, u32[]{:S(2)}, u32[]{:S(2)}) collective-permute-start(bf16[128,1024]{1,0:T(8,128)(2,1)} %get-tuple-element.1274), channel_id=1, source_target_pairs={{0,64},{64,128},{128,192},{1,65},{65,129},{129,193},{2,66},{66,130... | collective-permute-start | bytes 786440 | tf_op jit(solution)/shard_map/ppermute | solution.py:19
  62.1 8.0 %collective-permute-start.3 = (bf16[128,1024]{1,0:T(8,128)(2,1)}, bf16[128,1024]{1,0:T(8,128)(2,1)S(1)}, u32[]{:S(2)}, u32[]{:S(2)}) collective-permute-start(bf16[128,1024]{1,0:T(8,128)(2,1)} %get-tuple-element.1277), channel_id=1, source_target_pairs={{0,64},{64,128},{128,192},{1,65},{65,129},{129,193},{2,66},{66,130... | collective-permute-start | bytes 786440 | tf_op jit(solution)/shard_map/ppermute | solution.py:19
  74.8 16.7 %collective-permute-done.4 = bf16[128,1024]{1,0:T(8,128)(2,1)S(1)} collective-permute-done((bf16[128,1024]{1,0:T(8,128)(2,1)S(1)}, bf16[128,1024]{1,0:T(8,128)(2,1)S(1)}, u32[]{:S(2)}, u32[]{:S(2)}) %collective-permute-start.4) | collective-permute-done | bytes 262176 | tf_op jit(solution)/shard_map/ppermute | solution.py:19
  94.0 8.7 %collective-permute-done.5 = bf16[128,1024]{1,0:T(8,128)(2,1)S(1)} collective-permute-done((bf16[128,1024]{1,0:T(8,128)(2,1)}, bf16[128,1024]{1,0:T(8,128)(2,1)S(1)}, u32[]{:S(2)}, u32[]{:S(2)}) %collective-permute-start.5) | collective-permute-done | bytes 262176 | tf_op jit(solution)/shard_map/ppermute | solution.py:19
  105.3 62.3 %collective-permute-done.6 = bf16[128,1024]{1,0:T(8,128)(2,1)S(1)} collective-permute-done((bf16[128,1024]{1,0:T(8,128)(2,1)}, bf16[128,1024]{1,0:T(8,128)(2,1)S(1)}, u32[]{:S(2)}, u32[]{:S(2)}) %collective-permute-start.6) | collective-permute-done | bytes 262176 | tf_op jit(solution)/shard_map/ppermute | solution.py:19
  167.6 20.6 %conditional.29 = (bf16[128,1024]{1,0:T(8,128)(2,1)}, bf16[2,128,3072]{1,2,0:T(8,128)(2,1)}, bf16[2,128,1024]{2,1,0:T(8,128)(2,1)S(1)}, bf16[2,128,1024]{1,2,0:T(8,128)(2,1)S(1)}) conditional(s32[]{:T(128)} %convert_element_type.1133, (bf16[2,128,3072]{1,2,0:T(8,128)(2,1)}, bf16[2,128,1024]{2,1,0:T(8,128)(2,1)S(1)}, ...), branch_computations={%region_67.68_spmd, %region_68.74_spmd} | conditional | flops 2095847296 | bytes 59532540 | solution.py:270
  171.7 3.8 convolution_convert_fusion.37
  189.5 8.1 %collective-permute-done.7 = bf16[128,1024]{1,0:T(8,128)(2,1)S(1)} collective-permute-done((bf16[128,1024]{1,0:T(8,128)(2,1)}, bf16[128,1024]{1,0:T(8,128)(2,1)S(1)}, u32[]{:S(2)}, u32[]{:S(2)}) %collective-permute-start.7) | collective-permute-done | bytes 262176 | tf_op jit(solution)/shard_map/ppermute | solution.py:19
  197.6 15.9 %conditional.30 = ((bf16[2,128,3072]{1,2,0:T(8,128)(2,1)}, bf16[2,128,1024]{2,1,0:T(8,128)(2,1)S(1)}, bf16[2,128,1024]{1,2,0:T(8,128)(2,1)S(1)})) conditional(s32[]{:T(128)} %convert_element_type.1132, (bf16[2,128,3072]{1,2,0:T(8,128)(2,1)}, bf16[2,128,1024]{2,1,0:T(8,128)(2,1)S(1)}, bf16[2,128,1024]{1,2,0:T(8,128)(2,1)S(1)}) %tuple.196, ...), branch_computations={%region_74.75_spmd, %region_75.80_spmd} | conditional | flops 1286214912 | bytes 31606984 | solution.py:270
  201.6 3.8 convolution_convert_fusion.45
  214.2 3.4 convolution_bitcast_fusion.5
  217.7 6.0 pad_maximum_fusion
  223.8 358.9 %reduce-scatter.2.cloned.1.call-done = f32[1,16,4096]{2,1,0:T(8,128)} async-done(((f32[1,1024,4096]{2,1,0:T(8,128)}), f32[1,16,4096]{2,1,0:T(8,128)}) %reduce-scatter.2.cloned.1.call-update) | async-done | bytes 262160 | tf_op jit(solution)/shard_map/reduce_scatter | solution.py:24
  587.0 6.9 %psum.35 = f32[]{:T(128)} all-reduce(f32[]{:T(128)S(6)} %add.754), channel_id=1, replica_groups=mesh['section_0'=2,'section_1'=2,'dp_0'=2,'dp_1'=4,'dp_2'=8] {'section_0'}, use_global_device_ids=true, to_apply=%region_83.84 | all-reduce | flops 1 | bytes 8 | tf_op jit(solution)/shard_map/psum | solution.py:33
  593.9 3.1 psum.36
  597.0 5.5 psum.37
  602.5 8.3 %psum.38 = f32[]{:T(128)} all-reduce(f32[]{:T(128)} %psum.37), channel_id=1, replica_groups=mesh['section_0'=2,'section_1'=2,'dp_0'=2,'dp_1'=4,'dp_2'=8] {'dp_1'}, use_global_device_ids=true, to_apply=%region_86.87 | all-reduce | flops 1 | bytes 8 | tf_op jit(solution)/shard_map/psum | solution.py:33
  610.9 16.6 %psum.39 = f32[]{:T(128)} all-reduce(f32[]{:T(128)} %psum.38), channel_id=1, replica_groups=mesh['section_0'=2,'section_1'=2,'dp_0'=2,'dp_1'=4,'dp_2'=8] {'dp_2'}, use_global_device_ids=true, to_apply=%region_87.88 | all-reduce | flops 1 | bytes 8 | tf_op jit(solution)/shard_map/psum | solution.py:33
  (174 shorter events, 76.5 us)
Async XLA Ops:
  7.2 11.2 %copy-start = (bf16[1,256,3072]{2,1,0:T(8,128)(2,1)S(1)}, bf16[1,256,3072]{2,1,0:T(8,128)(2,1)}, u32[]{:S(2)}) copy-start(bf16[1,256,3072]{2,1,0:T(8,128)(2,1)} %param.50) | copy-start | bytes 4718596
  7.2 11.6 %copy-start.14 = (bf16[4,1024]{1,0:T(4,128)(2,1)S(1)}, bf16[4,1024]{1,0:T(4,128)(2,1)}, u32[]{:S(2)}) copy-start(bf16[4,1024]{1,0:T(4,128)(2,1)} %param.53) | copy-start | bytes 24580
  7.2 575.4 %reduce-scatter.2.cloned.1.call-start = ((), (), s32[]{:S(2)}) async-start(), calls=%async_computation.1 | async-start | bytes 17039360 | tf_op jit(solution)/shard_map/reduce_scatter | solution.py:24
  18.8 12.1 %copy-start.33 = (bf16[32,1024]{1,0:T(8,128)(2,1)S(1)}, bf16[32,1024]{1,0:T(8,128)(2,1)}, u32[]{:S(2)}) copy-start(bf16[32,1024]{1,0:T(8,128)(2,1)} %param.49) | copy-start | bytes 196612
  18.8 12.4 %copy-start.28 = (bf16[4,1024]{1,0:T(4,128)(2,1)S(1)}, bf16[4,1024]{1,0:T(4,128)(2,1)}, u32[]{:S(2)}) copy-start(bf16[4,1024]{1,0:T(4,128)(2,1)} %param.48) | copy-start | bytes 24580
  19.3 4.1 copy-start.2
  28.0 1.6 copy-start.3
  29.6 2.6 collective-permute-start
  41.9 3.6 collective-permute-start.1
  53.0 8.4 %collective-permute-start.2 = (bf16[128,1024]{1,0:T(8,128)(2,1)}, bf16[128,1024]{1,0:T(8,128)(2,1)S(1)}, u32[]{:S(2)}, u32[]{:S(2)}) collective-permute-start(bf16[128,1024]{1,0:T(8,128)(2,1)} %get-tuple-element.1274), channel_id=1, source_target_pairs={{0,64},{64,128},{128,192},{1,65},{65,129},{129,193},{2,66},{66,130... | collective-permute-start | bytes 786440 | tf_op jit(solution)/shard_map/ppermute | solution.py:19
  62.1 9.4 %collective-permute-start.3 = (bf16[128,1024]{1,0:T(8,128)(2,1)}, bf16[128,1024]{1,0:T(8,128)(2,1)S(1)}, u32[]{:S(2)}, u32[]{:S(2)}) collective-permute-start(bf16[128,1024]{1,0:T(8,128)(2,1)} %get-tuple-element.1277), channel_id=1, source_target_pairs={{0,64},{64,128},{128,192},{1,65},{65,129},{129,193},{2,66},{66,130... | collective-permute-start | bytes 786440 | tf_op jit(solution)/shard_map/ppermute | solution.py:19
  73.5 18.0 %collective-permute-start.4 = (bf16[128,1024]{1,0:T(8,128)(2,1)S(1)}, bf16[128,1024]{1,0:T(8,128)(2,1)S(1)}, u32[]{:S(2)}, u32[]{:S(2)}) collective-permute-start(bf16[128,1024]{1,0:T(8,128)(2,1)S(1)} %get-tuple-element.1283), channel_id=1, source_target_pairs={{64,0},{128,64},{192,128},{65,1},{129,65},{193,129},{66,2},{130,66... | collective-permute-start | bytes 786440 | tf_op jit(solution)/shard_map/ppermute | solution.py:19
  92.7 10.0 %collective-permute-start.5 = (bf16[128,1024]{1,0:T(8,128)(2,1)}, bf16[128,1024]{1,0:T(8,128)(2,1)S(1)}, u32[]{:S(2)}, u32[]{:S(2)}) collective-permute-start(bf16[128,1024]{1,0:T(8,128)(2,1)} %get-tuple-element.1287), channel_id=1, source_target_pairs={{64,0},{128,64},{192,128},{65,1},{129,65},{193,129},{66,2},{130,66... | collective-permute-start | bytes 786440 | tf_op jit(solution)/shard_map/ppermute | solution.py:19
  104.0 63.6 %collective-permute-start.6 = (bf16[128,1024]{1,0:T(8,128)(2,1)}, bf16[128,1024]{1,0:T(8,128)(2,1)S(1)}, u32[]{:S(2)}, u32[]{:S(2)}) collective-permute-start(bf16[128,1024]{1,0:T(8,128)(2,1)} %get-tuple-element.1291), channel_id=1, source_target_pairs={{64,0},{128,64},{192,128},{65,1},{129,65},{193,129},{66,2},{130,66... | collective-permute-start | bytes 786440 | tf_op jit(solution)/shard_map/ppermute | solution.py:19
  181.0 1.3 copy-start.23
  181.9 3.0 slice-start.6
  182.3 2.6 slice-start.7
  188.2 9.4 %collective-permute-start.7 = (bf16[128,1024]{1,0:T(8,128)(2,1)}, bf16[128,1024]{1,0:T(8,128)(2,1)S(1)}, u32[]{:S(2)}, u32[]{:S(2)}) collective-permute-start(bf16[128,1024]{1,0:T(8,128)(2,1)} %get-tuple-element.1295), channel_id=1, source_target_pairs={{64,0},{128,64},{192,128},{65,1},{129,65},{193,129},{66,2},{130,66... | collective-permute-start | bytes 786440 | tf_op jit(solution)/shard_map/ppermute | solution.py:19
  207.2 2.4 copy-start.13
  223.7 404.4 %copy-start.31 = (f32[1,16,1024]{2,1,0:T(8,128)S(1)}, f32[1,16,1024]{2,1,0:T(8,128)}, u32[]{:S(2)}) copy-start(f32[1,16,1024]{2,1,0:T(8,128)} %param.57) | copy-start | bytes 196612
  223.7 404.4 %copy-start.32 = (f32[1,16,1024]{2,1,0:T(8,128)S(1)}, f32[1,16,1024]{2,1,0:T(8,128)}, u32[]{:S(2)}) copy-start(f32[1,16,1024]{2,1,0:T(8,128)} %param.55) | copy-start | bytes 196612
  223.7 406.0 %copy-start.29 = (f32[1,16,3072]{2,1,0:T(8,128)S(1)}, f32[1,16,3072]{2,1,0:T(8,128)}, u32[]{:S(2)}) copy-start(f32[1,16,3072]{2,1,0:T(8,128)} %param.56) | copy-start | bytes 589828
  223.7 406.0 %copy-start.30 = (f32[1,16,3072]{2,1,0:T(8,128)S(1)}, f32[1,16,3072]{2,1,0:T(8,128)}, u32[]{:S(2)}) copy-start(f32[1,16,3072]{2,1,0:T(8,128)} %param.54) | copy-start | bytes 589828
  223.7 407.8 %copy-start.1 = (bf16[1,256,3072]{2,1,0:T(8,128)(2,1)S(1)}, bf16[1,256,3072]{2,1,0:T(8,128)(2,1)}, u32[]{:S(2)}) copy-start(bf16[1,256,3072]{2,1,0:T(8,128)(2,1)} %param.50) | copy-start | bytes 4718596
  (4 other events, 4.0 us)
Sparse Core Ops, SparseCore 0:
  223.9 358.7 reduce-scatter.1
where the time goes:
time: 647 us; the launch traced here: 639 us
  waiting for transfers between devices  458 us (71%)
  matrix products  47.1 us (7%)
  blocking collectives  40.5 us (6%)
  starting transfers between devices  23.8 us (4%)
  other arithmetic  20.6 us (3%)
  between operations  20.6 us (3%)
  local copies, waits for them, and re-layouts  19.7 us (3%)
  loops' own time  8.5 us (1%)
    reduce_scatter x1, waiting for transfers between devices, side_by_side(): lax.psum_scatter(both, axis, scatter_dimension=dim, tiled=True)  359 us
    ppermute x8, waiting for transfers between devices, passed_along(): return lax.ppermute(x, axis, pairs)  99 us
    psum x5, blocking collectives, over_axes(): x = lax.psum(x, axis)  40.5 us
    ppermute x8, starting transfers between devices, passed_along(): return lax.ppermute(x, axis, pairs)  23.8 us
    dot_general x5, matrix products, piece_a(): jnp.dot(normed, weight_qkv, preferred_element_type=jnp.float32)  17.9 us
  transfers between devices with their start and end apart: 9, of which 9 were waited for; matrix products, arithmetic and copies ran while one was open for 0% of the time, Pallas kernels for 0%

commit v1 on v0

v1 whole, which is shorter than its diff:
```python
import functools
import math

import jax
import jax.numpy as jnp
from jax import lax
from jax.experimental import pallas as pl
from jax.experimental.pallas import tpu as pltpu
from jax.sharding import Mesh
from jax.sharding import PartitionSpec as P

HEADS = 16
HEAD_DIM = 64
SECTION = ("section_0", "section_1")
DP = ("dp_0", "dp_1", "dp_2")
MESH = pl.DeviceIdType.MESH
F32 = jnp.float32
BF16 = jnp.bfloat16
D = 1024
SEQ = 128
NX = 4
NZ = 8
QB = 3 * D // NX
OB = D // NX
VMEM = pl.BlockSpec(memory_space=pltpu.VMEM)


def time_embed(step_ids, emb_width):
    half_dim = emb_width // 2
    frequency = jnp.exp(-math.log(10000.0) * jnp.arange(half_dim, dtype=jnp.float32) / half_dim)
    phases = step_ids.astype(jnp.float32)[:, None] * frequency[None, :]
    joined = jnp.concatenate([jnp.cos(phases), jnp.sin(phases)], axis=-1)
    return jax.nn.silu(joined).astype(jnp.bfloat16)


def embed_sample(latent_now, noise_now, step_now, camera_now, embed_in, camera_table):
    step_f = step_now.astype(jnp.float32)
    alpha_bar = jnp.cos((step_f / 1000.0 + 0.008) / 1.008 * (math.pi / 2.0)) ** 2
    noised = jnp.sqrt(alpha_bar) * latent_now.astype(jnp.float32) + jnp.sqrt(
        1.0 - alpha_bar
    ) * noise_now.astype(jnp.float32)
    features = lax.dot_general(
        noised.astype(jnp.bfloat16),
        embed_in,
        (((0,), (0,)), ((), ())),
        preferred_element_type=jnp.float32,
    )
    onehot = (
        camera_now[:, None] == jnp.arange(camera_table.shape[0], dtype=jnp.int32)[None, :]
    ).astype(jnp.bfloat16)
    camera_vec = jnp.dot(onehot, camera_table, preferred_element_type=jnp.float32)
    model_width = embed_in.shape[1]
    views = camera_now.shape[0]
    joined = features.reshape(views, -1, model_width) + camera_vec[:, None, :]
    return joined.reshape(-1, model_width).astype(jnp.bfloat16)


def dot_nn(a, b):
    return lax.dot_general(a, b, (((1,), (0,)), ((), ())), preferred_element_type=F32)


def dot_nt(a, b):
    return lax.dot_general(a, b, (((1,), (1,)), ((), ())), preferred_element_type=F32)


def dot_tn(a, b):
    return lax.dot_general(a, b, (((0,), (0,)), ((), ())), preferred_element_type=F32)


def lanes(start, size):
    return pl.ds(pl.multiple_of(start, 128), size)


def pipe_kernel(
    h0_ref, mod_ref, noise_ref, wqkv_ref, wout_ref, head_ref,
    nall, aall, ball, pall,
    h_scr, hn_scr, nrm_scr, att_scr, qkv_scr, p_scr, r_scr, g_scr, gs_scr,
    dqkv_scr, pc_scr, datt_scr, tmp_scr, mods, noi,
    h_send, h_recv, g_send, g_recv, sw_send, sw_recv, x_send, x_recv,
):
    s0 = lax.axis_index("section_0")
    s1 = lax.axis_index("section_1")
    d0 = lax.axis_index("dp_0")
    mx = lax.axis_index("dp_1")
    sec = 2 * s0 + s1

    def toward(step):
        other = sec + step
        o0 = lax.rem(lax.div(other + 4, 2), 2)
        o1 = lax.rem(other + 4, 2)
        crossing = (o0 + s0) - 2 * o0 * s0
        od = (d0 + crossing) - 2 * d0 * crossing
        return {"section_0": o0, "section_1": o1, "dp_0": od}

    nxt = toward(1)
    prv = toward(-1)
    partner = {"dp_0": 1 - d0}

    barrier = pltpu.get_barrier_semaphore()

    def greet(where):
        pl.semaphore_signal(barrier, inc=1, device_id=where, device_id_type=MESH)

    for d in range(1, NX):
        greet({"dp_1": lax.rem(mx + d, NX)})

    @pl.when(sec < 3)
    def _():
        greet(nxt)

    @pl.when(sec > 0)
    def _():
        greet(prv)

    @pl.when(s0 == 1)
    def _():
        greet(partner)

    pl.semaphore_wait(barrier, NX - 1 + lax.min(sec, 1) + lax.min(3 - sec, 1) + s0)

    def remote(src, dst, ssem, rsem, where):
        return pltpu.make_async_remote_copy(
            src_ref=src, dst_ref=dst, send_sem=ssem, recv_sem=rsem,
            device_id=where, device_id_type=MESH,
        )

    def swap_mod():
        return remote(mod_ref, mods, sw_send.at[0], sw_recv.at[0], partner)

    def swap_noise():
        return remote(noise_ref, noi, sw_send.at[1], sw_recv.at[1], partner)

    @pl.when(s0 == 1)
    def _():
        swap_mod().start()
        swap_noise().start()
        swap_mod().wait_recv()
        swap_noise().wait_recv()

    @pl.when(s0 == 0)
    def _():
        mods[...] = mod_ref[...]

    def h_copy(m):
        return remote(hn_scr.at[m], h_scr.at[m], h_send.at[m], h_recv.at[m], nxt)

    def g_copy(m):
        return remote(gs_scr.at[m], g_scr.at[m], g_send.at[m], g_recv.at[m], prv)

    def x_copies(m, which):
        rows = pl.ds(m * SEQ, SEQ)
        made = []
        for d in range(1, NX):
            to = lax.rem(mx + d, NX)
            where = {"dp_1": to}
            for k in which:
                src, dst = (
                    (nrm_scr.at[m], nall.at[mx, rows]),
                    (att_scr.at[m], aall.at[mx, rows]),
                    (dqkv_scr.at[m, :, lanes(to * QB, QB)], ball.at[mx, rows]),
                    (pc_scr.at[m, :, lanes(to * OB, OB)], pall.at[mx, rows]),
                )[k]
                made.append(remote(src, dst, x_send.at[m, d - 1, k], x_recv.at[m, d - 1, k], where))
        return made

    low = lax.broadcasted_iota(jnp.int32, (SEQ, 128), 1) < HEAD_DIM

    def both(tile):
        zero = jnp.zeros_like(tile)
        return jnp.concatenate([jnp.where(low, tile, zero), jnp.where(low, zero, tile)], axis=0)

    def merged(pair):
        return jnp.where(low, pair[:SEQ], pair[SEQ:])

    PAIRS = HEADS // 2
    GROUP = 4

    def over_pairs(body):
        def step(i, carry):
            for j in range(GROUP):
                body(i * GROUP + j)
            return carry

        lax.fori_loop(0, PAIRS // GROUP, step, 0)

    def forward(m, carry):
        @pl.when(sec == 0)
        def _():
            h_scr[m] = h0_ref[m]

        @pl.when(sec > 0)
        def _():
            h_copy(m).wait_recv()

        shift = mods[pl.ds(m * 8, 1), :]
        scale = mods[pl.ds(m * 8 + 1, 1), :]
        gate = mods[pl.ds(m * 8 + 2, 1), :]
        hf = h_scr[m].astype(F32)
        r = lax.rsqrt(jnp.mean(hf * hf, axis=-1, keepdims=True) + 1e-06)
        r_scr[m] = jnp.broadcast_to(r, (SEQ, 128))
        nrm_scr[m] = (hf * r * (1.0 + scale) + shift).astype(BF16)
        for n in range(6):
            cols = pl.ds(n * 512, 512)
            qkv_scr[m, :, cols] = dot_nn(nrm_scr[m], wqkv_ref[:, cols]).astype(BF16)

        def pair(j):
            q = qkv_scr[m, :, lanes(j * 128, 128)]
            k = qkv_scr[m, :, lanes(D + j * 128, 128)]
            v = qkv_scr[m, :, lanes(2 * D + j * 128, 128)]
            s = dot_nt(both(q), k) * (1.0 / math.sqrt(HEAD_DIM))
            s = jnp.exp(s - jnp.max(s, axis=-1, keepdims=True))
            p = s / jnp.sum(s, axis=-1, keepdims=True)
            p_scr[m, j] = p
            att_scr[m, :, lanes(j * 128, 128)] = merged(dot_nn(p.astype(BF16), v)).astype(BF16)

        over_pairs(pair)
        for n in range(2):
            cols = pl.ds(n * 512, 512)
            proj = dot_nn(att_scr[m], wout_ref[:, cols])
            hn_scr[m, :, cols] = (
                h_scr[m, :, cols].astype(F32) + gate[:, n * 512 : (n + 1) * 512] * proj
            ).astype(BF16)

        @pl.when(sec < 3)
        def _():
            h_copy(m).start()

        for copy in x_copies(m, (0, 1)):
            copy.start()
        rows = pl.ds(m * SEQ, SEQ)
        nall[mx, rows] = nrm_scr[m]
        aall[mx, rows] = att_scr[m]

        @pl.when(sec == 3)
        def _():
            ff = hn_scr[m].astype(F32)
            rr = lax.rsqrt(jnp.mean(ff * ff, axis=-1, keepdims=True) + 1e-06)
            predicted = dot_nt(head_ref[...], (ff * rr).astype(BF16))
            err = 2.0 * (predicted - noi[m])
            hi = err.astype(BF16)
            lo = (err - hi.astype(F32)).astype(BF16)
            dn = (dot_tn(hi, head_ref[...]) + dot_tn(lo, head_ref[...])).astype(BF16).astype(F32)
            inner = jnp.sum(dn * ff, axis=-1, keepdims=True) * (1.0 / D)
            g_scr[m] = (dn * rr - ff * (rr * rr * rr * inner)).astype(BF16)

        return carry

    lax.fori_loop(0, 2, forward, 0)

    def backward(m, carry):
        @pl.when(sec < 3)
        def _():
            g_copy(m).wait_recv()

        scale = mods[pl.ds(m * 8 + 1, 1), :]
        gate = mods[pl.ds(m * 8 + 2, 1), :]
        pc_scr[m] = (gate * g_scr[m].astype(F32)).astype(BF16)
        for copy in x_copies(m, (3,)):
            copy.start()
        for n in range(2):
            cols = pl.ds(n * 512, 512)
            datt_scr[:, cols] = dot_nt(pc_scr[m], wout_ref[cols, :]).astype(BF16)

        def pair(j):
            cq, ck, cv = lanes(j * 128, 128), lanes(D + j * 128, 128), lanes(2 * D + j * 128, 128)
            q2 = both(qkv_scr[m, :, cq])
            k = qkv_scr[m, :, ck]
            v = qkv_scr[m, :, cv]
            do2 = both(datt_scr[:, cq])
            p = p_scr[m, j]
            dv = dot_tn(p.astype(BF16), do2)
            dp = dot_nt(do2, v).astype(BF16).astype(F32)
            ds = p * (dp - jnp.sum(dp * p, axis=-1, keepdims=True))
            ds = (ds * (1.0 / math.sqrt(HEAD_DIM))).astype(BF16)
            dqkv_scr[m, :, cv] = dv.astype(BF16)
            dqkv_scr[m, :, cq] = merged(dot_nn(ds, k)).astype(BF16)
            dqkv_scr[m, :, ck] = dot_tn(ds, q2).astype(BF16)

        over_pairs(pair)
        for copy in x_copies(m, (2,)):
            copy.start()

        @pl.when(sec > 0)
        def _():
            for n in range(2):
                cols = pl.ds(n * 512, 512)
                tmp_scr[:, cols] = dot_nt(dqkv_scr[m], wqkv_ref[cols, :]).astype(BF16)
            hf = h_scr[m].astype(F32)
            r = r_scr[m][:, :1]
            u = tmp_scr[...].astype(F32) * (1.0 + scale)
            inner = jnp.sum(u * hf, axis=-1, keepdims=True) * (1.0 / D)
            dh = (u * r - hf * (r * r * r * inner)).astype(BF16).astype(F32)
            gs_scr[m] = (dh + g_scr[m].astype(F32)).astype(BF16)
            g_copy(m).start()

        rows = pl.ds(m * SEQ, SEQ)
        ball[mx, rows] = dqkv_scr[m, :, lanes(mx * QB, QB)]
        pall[mx, rows] = pc_scr[m, :, lanes(mx * OB, OB)]
        return carry

    lax.fori_loop(0, 2, backward, 0)

    def finish(m, carry):
        for copy in x_copies(m, (0, 1, 2, 3)):
            copy.wait()

        @pl.when(sec < 3)
        def _():
            h_copy(m).wait_send()

        @pl.when(sec > 0)
        def _():
            g_copy(m).wait_send()

        return carry

    lax.fori_loop(0, 2, finish, 0)

    @pl.when(s0 == 1)
    def _():
        swap_mod().wait_send()
        swap_noise().wait_send()


def run_pipe(h0, mod, noise, w_qkv, w_out, head):
    shape = jax.ShapeDtypeStruct
    dma = pltpu.SemaphoreType.DMA
    return pl.pallas_call(
        pipe_kernel,
        out_shape=(
            shape((NX, 2 * SEQ, D), BF16),
            shape((NX, 2 * SEQ, D), BF16),
            shape((NX, 2 * SEQ, QB), BF16),
            shape((NX, 2 * SEQ, OB), BF16),
        ),
        in_specs=[VMEM] * 6,
        out_specs=[VMEM] * 4,
        scratch_shapes=[
            pltpu.VMEM((2, SEQ, D), BF16),
            pltpu.VMEM((2, SEQ, D), BF16),
            pltpu.VMEM((2, SEQ, D), BF16),
            pltpu.VMEM((2, SEQ, D), BF16),
            pltpu.VMEM((2, SEQ, 3 * D), BF16),
            pltpu.VMEM((2, HEADS // 2, 2 * SEQ, SEQ), F32),
            pltpu.VMEM((2, SEQ, 128), F32),
            pltpu.VMEM((2, SEQ, D), BF16),
            pltpu.VMEM((2, SEQ, D), BF16),
            pltpu.VMEM((2, SEQ, 3 * D), BF16),
            pltpu.VMEM((2, SEQ, D), BF16),
            pltpu.VMEM((SEQ, D), BF16),
            pltpu.VMEM((SEQ, D), BF16),
            pltpu.VMEM((16, D), F32),
            pltpu.VMEM((2, 16, SEQ), F32),
            dma((2,)), dma((2,)), dma((2,)), dma((2,)), dma((2,)), dma((2,)),
            dma((2, NX - 1, 4)), dma((2, NX - 1, 4)),
        ],
        compiler_params=pltpu.CompilerParams(
            collective_id=0, has_side_effects=True, vmem_limit_bytes=50 * 2**20
        ),
        name="pipe",
    )(h0, mod, noise, w_qkv, w_out, head)


def reduce_kernel(
    g_ref, out_ref, sq_ref,
    zbuf, ysend, ybuf, tot, sqs, sqz, sqx, sqr,
    z_send, z_recv, y_send, y_recv, x_send, x_recv,
    qz_send, qz_recv, qx_send, qx_recv, qr_send, qr_recv,
):
    s0 = lax.axis_index("section_0")
    s1 = lax.axis_index("section_1")
    d0 = lax.axis_index("dp_0")
    mx = lax.axis_index("dp_1")
    mz = lax.axis_index("dp_2")

    def flip(a, by):
        return 1 - a if by else a

    z_peers = [{"dp_2": lax.rem(mz + d, NZ)} for d in range(1, NZ)]
    x_peers = [{"dp_1": lax.rem(mx + d, NX)} for d in range(1, NX)]
    r_peers = [
        {"section_0": flip(s0, c & 4), "section_1": flip(s1, c & 2), "dp_0": flip(d0, c & 1)}
        for c in range(1, 8)
    ]
    barrier = pltpu.get_barrier_semaphore()
    for where in z_peers + x_peers + r_peers:
        pl.semaphore_signal(barrier, inc=1, device_id=where, device_id_type=MESH)
    pl.semaphore_wait(barrier, 17)

    def remote(src, dst, ssem, rsem, where):
        return pltpu.make_async_remote_copy(
            src_ref=src, dst_ref=dst, send_sem=ssem, recv_sem=rsem,
            device_id=where, device_id_type=MESH,
        )

    z_copies = [
        remote(g_ref.at[:, where["dp_2"]], zbuf.at[i], z_send.at[i], z_recv.at[i], where)
        for i, where in enumerate(z_peers)
    ]
    for copy in z_copies:
        copy.start()
    for copy in z_copies:
        copy.wait_recv()

    def z_sum(i):
        acc = g_ref[i, mz].astype(F32)
        for d in range(NZ - 1):
            acc = acc + zbuf[d, i].astype(F32)
        return acc

    def to_send(i, carry):
        ysend[i] = z_sum((1 - d0) * NX + i)
        return carry

    lax.fori_loop(0, NX, to_send, 0)
    y_copy = remote(ysend, ybuf, y_send.at[0], y_recv.at[0], {"dp_0": 1 - d0})
    y_copy.start()

    def to_keep(i, carry):
        tot[i] = z_sum(d0 * NX + i)
        return carry

    lax.fori_loop(0, NX, to_keep, 0)
    y_copy.wait_recv()

    def add_up(i, acc):
        full = tot[i] + ybuf[i]
        tot[i] = full
        full = full * full
        for c in range(D // 128):
            part = full[:, c * 128 : (c + 1) * 128]
            acc = acc + part[:8] + part[8:]
        return acc

    sqs[0] = lax.fori_loop(0, NX, add_up, jnp.zeros((8, 128), F32))
    x_copies = [
        remote(tot.at[where["dp_1"]], out_ref.at[mx], x_send.at[i], x_recv.at[i], where)
        for i, where in enumerate(x_peers)
    ]

    def sum_over(peers, src, buf, ssem, rsem):
        copies = [
            remote(src, buf.at[i], ssem.at[i], rsem.at[i], where) for i, where in enumerate(peers)
        ]
        for copy in copies:
            copy.start()
        return copies

    def take(copies, src, buf):
        for copy in copies:
            copy.wait_recv()
        acc = src[...]
        for i in range(len(copies)):
            acc = acc + buf[i]
        return acc

    qz = sum_over(z_peers, sqs.at[0], sqz, qz_send, qz_recv)
    for copy in x_copies:
        copy.start()
    out_ref[mx] = tot[mx]
    sqs[1] = take(qz, sqs.at[0], sqz)
    qx = sum_over(x_peers, sqs.at[1], sqx, qx_send, qx_recv)
    sqs[2] = take(qx, sqs.at[1], sqx)
    qr = sum_over(r_peers, sqs.at[2], sqr, qr_send, qr_recv)
    sq_ref[...] = take(qr, sqs.at[2], sqr)
    for copy in x_copies:
        copy.wait_recv()
    for copy in z_copies + [y_copy] + x_copies + qz + qx + qr:
        copy.wait_send()


def run_reduce(grad):
    shape = jax.ShapeDtypeStruct
    dma = pltpu.SemaphoreType.DMA
    return pl.pallas_call(
        reduce_kernel,
        out_shape=(shape((NX, 16, D), F32), shape((8, 128), F32)),
        in_specs=[VMEM],
        out_specs=[VMEM, VMEM],
        scratch_shapes=[
            pltpu.VMEM((NZ - 1, 8, 16, D), BF16),
            pltpu.VMEM((NX, 16, D), F32),
            pltpu.VMEM((NX, 16, D), F32),
            pltpu.VMEM((NX, 16, D), F32),
            pltpu.VMEM((3, 8, 128), F32),
            pltpu.VMEM((NZ - 1, 8, 128), F32),
            pltpu.VMEM((NX - 1, 8, 128), F32),
            pltpu.VMEM((7, 8, 128), F32),
            dma((NZ - 1,)), dma((NZ - 1,)), dma((1,)), dma((1,)), dma((NX - 1,)), dma((NX - 1,)),
            dma((NZ - 1,)), dma((NZ - 1,)), dma((NX - 1,)), dma((NX - 1,)), dma((7,)), dma((7,)),
        ],
        compiler_params=pltpu.CompilerParams(
            collective_id=1, has_side_effects=True, vmem_limit_bytes=32 * 2**20
        ),
        name="reduce",
    )(grad)


def optimizer_step(gradient, moment, second, factor):
    normalized = gradient * factor
    moment_new = 0.9 * moment + 0.1 * normalized
    second_new = 0.99 * second + 0.01 * normalized * normalized
    return (moment_new / (jnp.sqrt(second_new) + 1e-08), moment_new, second_new)


def local(
    latents,
    noise,
    timesteps,
    cameras,
    embed_in,
    camera_table,
    w_mod,
    w_qkv,
    w_out,
    head_out,
    moment_qkv,
    moment_out,
    second_qkv,
    second_out,
):
    time_emb = time_embed(timesteps, w_mod.shape[1])
    modulation = jnp.dot(time_emb, w_mod[0], preferred_element_type=jnp.float32)
    mod = jnp.pad(modulation.reshape(2, 3, D), ((0, 0), (0, 5), (0, 0))).reshape(16, D)
    h0 = jax.vmap(embed_sample, in_axes=(0, 0, 0, 0, None, None))(
        latents, noise, timesteps, cameras, embed_in, camera_table
    )
    noise_rows = jnp.pad(noise.astype(F32), ((0, 0), (0, 12), (0, 0)))
    head = jnp.pad(head_out, ((0, 12), (0, 0)))
    nall, aall, ball, pall = run_pipe(h0, mod, noise_rows, w_qkv[0], w_out[0], head)
    rows = NX * 2 * SEQ
    grad = jnp.concatenate(
        [
            dot_tn(nall.reshape(rows, D), ball.reshape(rows, QB)).astype(BF16),
            dot_tn(aall.reshape(rows, D), pall.reshape(rows, OB)).astype(BF16),
        ],
        axis=1,
    )
    shard, squares = run_reduce(grad.reshape(8, NZ, 16, D))
    factor = lax.rsqrt(jnp.sum(squares) / 16777216.0 + 1e-12)
    qkv_shard = jnp.transpose(shard[:, :, :QB], (1, 0, 2)).reshape(1, 16, 3 * D)
    out_shard = jnp.transpose(shard[:, :, QB:], (1, 0, 2)).reshape(1, 16, D)
    update_qkv, new_moment_qkv, new_second_qkv = optimizer_step(
        qkv_shard, moment_qkv, second_qkv, factor
    )
    update_out, new_moment_out, new_second_out = optimizer_step(
        out_shard, moment_out, second_out, factor
    )
    return (update_qkv, update_out, new_moment_qkv, new_moment_out, new_second_qkv, new_second_out)


def solution(mesh):
    torus = Mesh(
        mesh.devices.reshape(2, 2, 2, 4, 8), ("section_0", "section_1", "dp_0", "dp_1", "dp_2")
    )
    return jax.shard_map(
        local,
        mesh=torus,
        in_specs=(
            P(DP, None, None),
            P(DP, None, None),
            P(DP),
            P(DP, None),
            P(),
            P(),
            P(SECTION, None, None),
            P(SECTION, None, None),
            P(SECTION, None, None),
            P(),
            P(SECTION, DP, None),
            P(SECTION, DP, None),
            P(SECTION, DP, None),
            P(SECTION, DP, None),
        ),
        out_specs=(
            P(SECTION, DP, None),
            P(SECTION, DP, None),
            P(SECTION, DP, None),
            P(SECTION, DP, None),
            P(SECTION, DP, None),
            P(SECTION, DP, None),
        ),
        check_vma=False,
    )
```

time: 647 us -> 190 us (0.29)
  waiting for transfers between devices: 458 us -> 0 us
  Pallas kernels: 0 us -> 169 us
  blocking collectives: 40.5 us -> 0 us
  matrix products: 47.1 us -> 6.89 us
  starting transfers between devices: 23.8 us -> 0 us
  between operations: 20.6 us -> 1.6 us
  other arithmetic: 20.6 us -> 4.5 us
  local copies, waits for them, and re-layouts: 19.7 us -> 5.92 us
  loops' own time: 8.5 us -> 0 us
    reduce_scatter x1 -> x0, waiting for transfers between devices: 359 us -> none  [side_by_side(): lax.psum_scatter(both, axis, scatter_dimension=dim, tiled=True)]
    pallas_call x0 -> x2, Pallas kernels: none -> 169 us  [the longest x1 86.2 us: run_reduce(): pl.pallas_call(reduce_kernel, out_shape=(shape((NX, 16, D), F32), shape((...]
    ppermute x8 -> x0, waiting for transfers between devices: 99 us -> none  [passed_along(): return lax.ppermute(x, axis, pairs)]
    psum x5 -> x0, blocking collectives: 40.5 us -> none  [over_axes(): x = lax.psum(x, axis)]
    dot_general x25 -> x2, matrix products: 38.8 us -> 4.36 us  [dot_tn(): lax.dot_general(a, b, (((0,), (0,)), ((), ())), preferred_element_type=F32)]
    ppermute x8 -> x0, starting transfers between devices: 23.8 us -> none  [passed_along(): return lax.ppermute(x, axis, pairs)]
    another operation x11 -> x0, loops' own time: 8.5 us -> none  [the longest x4 6.97 us: local(): sent_act, buffers = lax.cond(is_active, active, resting, buffers)]
  transfers between devices with their start and end apart: 9 -> 0, of which waited for: 9 -> 0; matrix products, arithmetic and copies ran while one was open for 0% -> 0% of each run, Pallas kernels for 0% -> 0%
where the time goes in v1:
time: 190 us; the launch traced here: 188 us
  Pallas kernels  169 us (89%)
  matrix products  6.89 us (4%)
  local copies, waits for them, and re-layouts  5.92 us (3%)
  other arithmetic  4.5 us (2%)
    pallas_call x1, Pallas kernels, run_reduce(): pl.pallas_call(reduce_kernel, out_shape=(shape((NX, 16, D), F32), shape((...  86.2 us
    pallas_call x1, Pallas kernels, run_pipe(): pl.pallas_call(pipe_kernel, out_shape=(shape((NX, 2 * SEQ, D), BF16), sha...  82.7 us
    dot_general x2, matrix products, dot_tn(): lax.dot_general(a, b, (((0,), (0,)), ((), ())), preferred_element_type=F32)  4.36 us

profile of v1, /device:TPU:8, one launch (start us, length us, event | category | flops | bytes accessed | tf_op | source)
XLA Modules:
  0.0 187.8 jit_solution(7366479775283408281)
XLA Ops:
  0.6 0.0 copy-start
  0.6 0.8 copy-done
  1.5 0.9 fusion.4
  2.4 0.1 add.56
  2.5 0.7 fusion.17
  3.2 0.0 copy-start.8
  3.2 1.1 fusion.1.h0_ref
  4.3 0.0 copy-start.5
  4.4 1.7 copy.25
  6.1 0.1 multiply_cosine_fusion
  6.2 0.5 fusion.11
  6.8 82.7 %pipe.1 = (bf16[4,256,1024]{2,1,0:T(8,128)(2,1)}, bf16[4,256,1024]{2,1,0:T(8,128)(2,1)}, bf16[4,256,768]{2,1,0:T(8,128)(2,1)S(1)}, bf16[4,256,256]{2,1,0:T(8,128)(2,1)S(1)}) custom-call(bf16[2,128,1024]{2,1,0:T(8,128)(2,1)S(1)} %fusion.1.h0_ref, f32[16,1024]{1,0:T(8,128)S(1)} %pad_bitcast_fusion.mod_ref, f32[2,16,128]{2,1,0:T(8,128)S(1)} %pad.13.noise_ref, ...), custom_call_target="tpu_custom_call" | custom-call | tf_op jit(solution)/shard_map/pipe/pallas_call | solution.py:328
  89.5 2.5 %fusion = bf16[1024,256]{0,1:T(8,128)(2,1)S(1)} fusion(bf16[4,256,1024]{2,1,0:T(8,128)(2,1)} %get-tuple-element.14, bf16[4,256,256]{2,1,0:T(8,128)(2,1)S(1)} %get-tuple-element.15), kind=kOutput, calls=%fused_computation.4 | convolution fusion | flops 537133056 | bytes 3145728 | tf_op jit(solution)/shard_map/dot_general | solution.py:67
  92.1 1.9 bitcast_convert_fusion
  93.9 1.5 pad_maximum_fusion
  95.4 2.9 %copy.29 = bf16[1024,1024]{1,0:T(8,128)(2,1)S(1)} copy(bf16[1024,1024]{0,1:T(8,128)(2,1)} %pad_maximum_fusion) | data formatting | bytes 4194304 | tf_op jit(solution)/shard_map/concatenate | solution.py:532
  98.3 0.0 copy-start.2
  98.3 0.0 copy-start.3
  98.3 86.2 %reduce.1 = (f32[4,16,1024]{2,1,0:T(8,128)S(1)}, f32[8,128]{1,0:T(8,128)S(1)}) custom-call(bf16[8,8,16,1024]{3,2,1,0:T(8,128)(2,1)S(1)} %bitcast.35), custom_call_target="tpu_custom_call" | custom-call | tf_op jit(solution)/shard_map/reduce/pallas_call | solution.py:475
  184.6 0.6 reduce_sum.9
  185.9 0.1 copy.30
  186.0 0.1 mul.206
  186.1 0.9 add_divide_fusion
  187.1 0.7 add_divide_fusion.1
  (22 shorter events, 0.2 us)
Async XLA Ops:
  0.6 0.8 copy-start
  3.2 2.9 %copy-start.8 = (s32[2]{0:T(128)S(1)}, s32[2]{0:T(128)}, u32[]{:S(2)}) copy-start(s32[2]{0:T(128)} %param.16) | copy-start | bytes 28
  4.3 2.4 %copy-start.5 = (bf16[2,4,128]{2,1,0:T(4,128)(2,1)S(1)}, bf16[2,4,128]{2,1,0:T(4,128)(2,1)}, u32[]{:S(2)}) copy-start(bf16[2,4,128]{2,1,0:T(4,128)(2,1)} %param.15) | copy-start | bytes 6148
  4.4 2.5 %copy-start.6 = (bf16[4,1024]{1,0:T(4,128)(2,1)S(1)}, bf16[4,1024]{1,0:T(4,128)(2,1)}, u32[]{:S(2)}) copy-start(bf16[4,1024]{1,0:T(4,128)(2,1)} %param.23) | copy-start | bytes 24580
  89.5 2.5 %copy-start.7 = (bf16[4,256,1024]{2,1,0:T(8,128)(2,1)S(1)}, bf16[4,256,1024]{2,1,0:T(8,128)(2,1)}, u32[]{:S(2)}) copy-start(bf16[4,256,1024]{2,1,0:T(8,128)(2,1)} %get-tuple-element.12) | copy-start | bytes 6291460
  98.3 87.8 %copy-start.1 = (f32[1,16,3072]{2,1,0:T(8,128)S(1)}, f32[1,16,3072]{2,1,0:T(8,128)}, u32[]{:S(2)}) copy-start(f32[1,16,3072]{2,1,0:T(8,128)} %param.26) | copy-start | bytes 589828
  98.3 87.8 %copy-start.2 = (f32[1,16,3072]{2,1,0:T(8,128)S(1)}, f32[1,16,3072]{2,1,0:T(8,128)}, u32[]{:S(2)}) copy-start(f32[1,16,3072]{2,1,0:T(8,128)} %param.24) | copy-start | bytes 589828
  98.3 88.8 %copy-start.3 = (f32[1,16,1024]{2,1,0:T(8,128)S(1)}, f32[1,16,1024]{2,1,0:T(8,128)}, u32[]{:S(2)}) copy-start(f32[1,16,1024]{2,1,0:T(8,128)} %param.27) | copy-start | bytes 196612
  98.3 88.8 %copy-start.4 = (f32[1,16,1024]{2,1,0:T(8,128)S(1)}, f32[1,16,1024]{2,1,0:T(8,128)}, u32[]{:S(2)}) copy-start(f32[1,16,1024]{2,1,0:T(8,128)} %param.25) | copy-start | bytes 196612

commit v2 on v1

v2 whole, which is shorter than its diff:
```python
import functools
import math

import jax
import jax.numpy as jnp
from jax import lax
from jax.experimental import pallas as pl
from jax.experimental.pallas import tpu as pltpu
from jax.sharding import Mesh
from jax.sharding import PartitionSpec as P

HEADS = 16
HEAD_DIM = 64
SECTION = ("section_0", "section_1")
DP = ("dp_0", "dp_1", "dp_2")
MESH = pl.DeviceIdType.MESH
F32 = jnp.float32
BF16 = jnp.bfloat16
D = 1024
SEQ = 128
NX = 4
NZ = 8
QB = 3 * D // NX
OB = D // NX
VMEM = pl.BlockSpec(memory_space=pltpu.VMEM)
ANY = pl.BlockSpec(memory_space=pl.ANY)


def time_embed(step_ids, emb_width):
    half_dim = emb_width // 2
    frequency = jnp.exp(-math.log(10000.0) * jnp.arange(half_dim, dtype=jnp.float32) / half_dim)
    phases = step_ids.astype(jnp.float32)[:, None] * frequency[None, :]
    joined = jnp.concatenate([jnp.cos(phases), jnp.sin(phases)], axis=-1)
    return jax.nn.silu(joined).astype(jnp.bfloat16)


def embed_sample(latent_now, noise_now, step_now, camera_now, embed_in, camera_table):
    step_f = step_now.astype(jnp.float32)
    alpha_bar = jnp.cos((step_f / 1000.0 + 0.008) / 1.008 * (math.pi / 2.0)) ** 2
    noised = jnp.sqrt(alpha_bar) * latent_now.astype(jnp.float32) + jnp.sqrt(
        1.0 - alpha_bar
    ) * noise_now.astype(jnp.float32)
    features = lax.dot_general(
        noised.astype(jnp.bfloat16),
        embed_in,
        (((0,), (0,)), ((), ())),
        preferred_element_type=jnp.float32,
    )
    onehot = (
        camera_now[:, None] == jnp.arange(camera_table.shape[0], dtype=jnp.int32)[None, :]
    ).astype(jnp.bfloat16)
    camera_vec = jnp.dot(onehot, camera_table, preferred_element_type=jnp.float32)
    model_width = embed_in.shape[1]
    views = camera_now.shape[0]
    joined = features.reshape(views, -1, model_width) + camera_vec[:, None, :]
    return joined.reshape(-1, model_width).astype(jnp.bfloat16)


def dot_nn(a, b):
    return lax.dot_general(a, b, (((1,), (0,)), ((), ())), preferred_element_type=F32)


def dot_nt(a, b):
    return lax.dot_general(a, b, (((1,), (1,)), ((), ())), preferred_element_type=F32)


def dot_tn(a, b):
    return lax.dot_general(a, b, (((0,), (0,)), ((), ())), preferred_element_type=F32)


def lanes(start, size):
    return pl.ds(pl.multiple_of(start, 128), size)


def step_kernel(
    h0_ref, mod_ref, noise_ref, wqkv_hbm, wout_hbm, head_ref,
    outq_ref, outo_ref, factor_ref,
    wqkv_ref, wout_ref, wqkv_t, wout_t, nall, aall, ball, pall, n_t, a_t,
    h_scr, hn_scr, nrm_scr, att_scr, qkv_scr, p_scr, r_scr, g_scr, gs_scr,
    dqkv_scr, pc_scr, datt_scr, tmp_scr, mods, noi,
    up_out, up_in, dn_out, dn_in, summed, y_out, y_in, totq, toto, sqs, sqz, sqx, sqr,
    h_send, h_recv, g_send, g_recv, sw_send, sw_recv, x_send, x_recv,
    up_send, up_recv, dn_send, dn_recv, y_send, y_recv, o_send, o_recv,
    qz_send, qz_recv, qx_send, qx_recv, qr_send, qr_recv, w_sem,
):
    w_copies = [
        pltpu.make_async_copy(wqkv_hbm, wqkv_ref, w_sem.at[0]),
        pltpu.make_async_copy(wout_hbm, wout_ref, w_sem.at[1]),
    ]
    for copy in w_copies:
        copy.start()
    s0 = lax.axis_index("section_0")
    s1 = lax.axis_index("section_1")
    d0 = lax.axis_index("dp_0")
    mx = lax.axis_index("dp_1")
    mz = lax.axis_index("dp_2")
    sec = 2 * s0 + s1

    def toward(step):
        other = sec + step
        o0 = lax.rem(lax.div(other + 4, 2), 2)
        o1 = lax.rem(other + 4, 2)
        crossing = (o0 + s0) - 2 * o0 * s0
        od = (d0 + crossing) - 2 * d0 * crossing
        return {"section_0": o0, "section_1": o1, "dp_0": od}

    nxt = toward(1)
    prv = toward(-1)
    partner = {"dp_0": 1 - d0}

    barrier = pltpu.get_barrier_semaphore()

    def greet(where):
        pl.semaphore_signal(barrier, inc=1, device_id=where, device_id_type=MESH)

    def flip(a, by):
        return 1 - a if by else a

    z_peers = [{"dp_2": lax.rem(mz + d, NZ)} for d in range(1, NZ)]
    x_peers = [{"dp_1": lax.rem(mx + d, NX)} for d in range(1, NX)]
    r_peers = [
        {"section_0": flip(s0, c & 4), "section_1": flip(s1, c & 2), "dp_0": flip(d0, c & 1)}
        for c in range(1, 8)
    ]
    for where in z_peers + x_peers + r_peers:
        greet(where)

    @pl.when(sec < 3)
    def _():
        greet(nxt)

    @pl.when(sec > 0)
    def _():
        greet(prv)

    pl.semaphore_wait(barrier, 17 + lax.min(sec, 1) + lax.min(3 - sec, 1))

    def remote(src, dst, ssem, rsem, where):
        return pltpu.make_async_remote_copy(
            src_ref=src, dst_ref=dst, send_sem=ssem, recv_sem=rsem,
            device_id=where, device_id_type=MESH,
        )

    def swap_mod():
        return remote(mod_ref, mods, sw_send.at[0], sw_recv.at[0], partner)

    def swap_noise():
        return remote(noise_ref, noi, sw_send.at[1], sw_recv.at[1], partner)

    @pl.when(s0 == 1)
    def _():
        swap_mod().start()
        swap_noise().start()
        swap_mod().wait_recv()
        swap_noise().wait_recv()

    @pl.when(s0 == 0)
    def _():
        mods[...] = mod_ref[...]

    def h_copy(m, n):
        cols = pl.ds(n * 512, 512)
        return remote(
            hn_scr.at[m, :, cols], h_scr.at[m, :, cols], h_send.at[m, n], h_recv.at[m, n], nxt
        )

    def g_copy(m):
        return remote(gs_scr.at[m], g_scr.at[m], g_send.at[m], g_recv.at[m], prv)

    def rows_of(src, m):
        return pl.ds(pl.multiple_of(src * 2 * SEQ + m * SEQ, SEQ), SEQ)

    def x_copy(m, d, k):
        to = lax.rem(mx + d, NX)
        rows = rows_of(mx, m)
        src, dst = (
            (nrm_scr.at[m], nall.at[rows]),
            (att_scr.at[m], aall.at[rows]),
            (pc_scr.at[m, :, lanes(to * OB, OB)], pall.at[rows]),
        )[k] if k < 3 else (
            dqkv_scr.at[m, :, lanes(to * QB + (k - 3) * OB, OB)],
            ball.at[rows, pl.ds((k - 3) * OB, OB)],
        )
        return remote(src, dst, x_send.at[m, d - 1, k], x_recv.at[m, d - 1, k], {"dp_1": to})

    def act_copies(m):
        return [x_copy(m, d, k) for k in (0, 1) for d in (1, 3)]

    def cot_copies(m, k):
        return [x_copy(m, d, k) for d in (1, 2, 3)]

    def relays(m):
        left, right = lax.rem(mx + 3, NX), lax.rem(mx + 1, NX)
        nrows, arows = rows_of(left, m), rows_of(right, m)
        return [
            remote(
                nall.at[nrows], nall.at[nrows], x_send.at[m, 1, 0], x_recv.at[m, 1, 0],
                {"dp_1": right},
            ),
            remote(
                aall.at[arows], aall.at[arows], x_send.at[m, 1, 1], x_recv.at[m, 1, 1],
                {"dp_1": left},
            ),
        ]

    def relay(m):
        x_copy(m, 1, 0).wait_recv()
        x_copy(m, 3, 1).wait_recv()
        for copy in relays(m):
            copy.start()

    low = lax.broadcasted_iota(jnp.int32, (SEQ, 128), 1) < HEAD_DIM

    def both(tile):
        zero = jnp.zeros_like(tile)
        return jnp.concatenate([jnp.where(low, tile, zero), jnp.where(low, zero, tile)], axis=0)

    def merged(pair):
        return jnp.where(low, pair[:SEQ], pair[SEQ:])

    PAIRS = HEADS // 2
    GROUP = 4

    def over_pairs(body):
        def step(i, carry):
            for j in range(GROUP):
                body(i * GROUP + j)
            return carry

        lax.fori_loop(0, PAIRS // GROUP, step, 0)

    def forward(m, carry):
        @pl.when(sec == 0)
        def _():
            h_scr[m] = h0_ref[m]

        @pl.when(sec > 0)
        def _():
            h_copy(m, 0).wait_recv()
            h_copy(m, 1).wait_recv()

        shift = mods[pl.ds(m, 1), pl.ds(0, D)]
        scale = mods[pl.ds(m, 1), pl.ds(D, D)]
        gate = mods[pl.ds(m, 1), pl.ds(2 * D, D)]
        hf = h_scr[m].astype(F32)
        r = lax.rsqrt(jnp.mean(hf * hf, axis=-1, keepdims=True) + 1e-06)
        r_scr[m] = jnp.broadcast_to(r, (SEQ, 128))
        nrm_scr[m] = (hf * r * (1.0 + scale) + shift).astype(BF16)
        for n in range(6):
            cols = pl.ds(n * 512, 512)
            qkv_scr[m, :, cols] = dot_nn(nrm_scr[m], wqkv_ref[:, cols]).astype(BF16)

        def pair(j):
            q = qkv_scr[m, :, lanes(j * 128, 128)]
            k = qkv_scr[m, :, lanes(D + j * 128, 128)]
            v = qkv_scr[m, :, lanes(2 * D + j * 128, 128)]
            s = dot_nt(both(q), k) * (1.0 / math.sqrt(HEAD_DIM))
            s = jnp.exp(s - jnp.max(s, axis=-1, keepdims=True))
            p = s / jnp.sum(s, axis=-1, keepdims=True)
            p_scr[m, j] = p
            att_scr[m, :, lanes(j * 128, 128)] = merged(dot_nn(p.astype(BF16), v)).astype(BF16)

        over_pairs(pair)
        for n in range(2):
            cols = pl.ds(n * 512, 512)
            proj = dot_nn(att_scr[m], wout_ref[:, cols])
            hn_scr[m, :, cols] = (
                h_scr[m, :, cols].astype(F32) + gate[:, n * 512 : (n + 1) * 512] * proj
            ).astype(BF16)

            @pl.when(sec < 3)
            def _():
                h_copy(m, n).start()

        for copy in act_copies(m):
            copy.start()
        rows = rows_of(mx, m)
        nall[rows] = nrm_scr[m]
        aall[rows] = att_scr[m]

        @pl.when(sec == 3)
        def _():
            ff = hn_scr[m].astype(F32)
            rr = lax.rsqrt(jnp.mean(ff * ff, axis=-1, keepdims=True) + 1e-06)
            predicted = dot_nt(head_ref[...], (ff * rr).astype(BF16))
            err = 2.0 * (predicted - noi[m])
            hi = err.astype(BF16)
            lo = (err - hi.astype(F32)).astype(BF16)
            dn = (dot_tn(hi, head_ref[...]) + dot_tn(lo, head_ref[...])).astype(BF16).astype(F32)
            inner = jnp.sum(dn * ff, axis=-1, keepdims=True) * (1.0 / D)
            g_scr[m] = (dn * rr - ff * (rr * rr * rr * inner)).astype(BF16)

        return carry

    def turn_weights():
        def block(i, carry):
            here = lanes(i * 128, 128)
            for src, dst, tiles in ((wqkv_ref, wqkv_t, 24), (wout_ref, wout_t, 8)):
                for g in range(tiles):
                    dst[pl.ds(g * 128, 128), here] = jnp.transpose(src[here, pl.ds(g * 128, 128)])
            return carry

        lax.fori_loop(0, 8, block, 0)

    for copy in w_copies:
        copy.wait()

    @pl.when(s0 == 1)
    def _():
        turn_weights()

    lax.fori_loop(0, 2, forward, 0)

    def turn():
        def arrived(m, carry):
            x_copy(m, 3, 0).wait_recv()
            x_copy(m, 1, 1).wait_recv()
            for copy in relays(m):
                copy.wait_recv()
            return carry

        lax.fori_loop(0, 2, arrived, 0)

        def block(i, carry):
            here = lanes(i * SEQ, SEQ)
            for src, dst in ((nall, n_t), (aall, a_t)):
                for g in range(8):
                    tile = src[here, pl.ds(g * 128, 128)]
                    dst[g, :, :, here] = jnp.transpose(tile).reshape(NZ, 16, SEQ)
            return carry

        lax.fori_loop(0, 2 * NX, block, 0)

    @pl.when(sec < 3)
    def _():
        relay(0)

    @pl.when(s0 == 0)
    def _():
        relay(1)
        turn_weights()
        turn()

    def backward(m, carry):
        @pl.when(sec < 3)
        def _():
            g_copy(m).wait_recv()

        scale = mods[pl.ds(m, 1), pl.ds(D, D)]
        gate = mods[pl.ds(m, 1), pl.ds(2 * D, D)]
        pc_scr[m] = (gate * g_scr[m].astype(F32)).astype(BF16)
        for copy in cot_copies(m, 2):
            copy.start()
        for n in range(2):
            cols = pl.ds(n * 512, 512)
            datt_scr[:, cols] = dot_nn(pc_scr[m], wout_t[:, cols]).astype(BF16)

        def pair(j):
            cq, ck, cv = lanes(j * 128, 128), lanes(D + j * 128, 128), lanes(2 * D + j * 128, 128)
            q2 = both(qkv_scr[m, :, cq])
            k = qkv_scr[m, :, ck]
            v = qkv_scr[m, :, cv]
            do2 = both(datt_scr[:, cq])
            p = p_scr[m, j]
            dv = dot_tn(p.astype(BF16), do2)
            dp = dot_nt(do2, v).astype(BF16).astype(F32)
            ds = p * (dp - jnp.sum(dp * p, axis=-1, keepdims=True))
            ds = (ds * (1.0 / math.sqrt(HEAD_DIM))).astype(BF16)
            dqkv_scr[m, :, cv] = dv.astype(BF16)
            dqkv_scr[m, :, cq] = merged(dot_nn(ds, k)).astype(BF16)
            dqkv_scr[m, :, ck] = dot_tn(ds, q2).astype(BF16)

        over_pairs(pair)
        for k in (3, 4, 5):
            for copy in cot_copies(m, k):
                copy.start()

        @pl.when(sec > 0)
        def _():
            for n in range(2):
                cols = pl.ds(n * 512, 512)
                tmp_scr[:, cols] = dot_nn(dqkv_scr[m], wqkv_t[:, cols]).astype(BF16)
            hf = h_scr[m].astype(F32)
            r = r_scr[m][:, :1]
            u = tmp_scr[...].astype(F32) * (1.0 + scale)
            inner = jnp.sum(u * hf, axis=-1, keepdims=True) * (1.0 / D)
            dh = (u * r - hf * (r * r * r * inner)).astype(BF16).astype(F32)
            gs_scr[m] = (dh + g_scr[m].astype(F32)).astype(BF16)
            g_copy(m).start()

        rows = rows_of(mx, m)
        ball[rows] = dqkv_scr[m, :, lanes(mx * QB, QB)]
        pall[rows] = pc_scr[m, :, lanes(mx * OB, OB)]

        @pl.when((sec == 2) & (m == 0))
        def _():
            relay(1)

        return carry

    lax.fori_loop(0, 2, backward, 0)

    @pl.when(sec == 3)
    def _():
        relay(0)
        relay(1)

    @pl.when(s0 == 1)
    def _():
        turn()

    def exchanged(quarter):
        def arrive(m, carry):
            for copy in cot_copies(m, 2 + quarter):
                copy.wait_recv()
            return carry

        lax.fori_loop(0, 2, arrive, 0)

    def partial(dest, quarter):
        left = (n_t if quarter else a_t)[:, dest].reshape(8 * 16, NX * 2 * SEQ)
        if quarter == 0:
            return dot_nn(left, pall[...])
        return dot_nn(left, ball[:, pl.ds((quarter - 1) * OB, OB)])

    z_up = {"dp_2": lax.rem(mz + 1, NZ)}
    z_dn = {"dp_2": lax.rem(mz + NZ - 1, NZ)}

    def ring_copy(up, t, quarter):
        k = 4 * quarter + t
        if up:
            return remote(up_out.at[k], up_in.at[k], up_send.at[k], up_recv.at[k], z_up)
        return remote(dn_out.at[k], dn_in.at[k], dn_send.at[k], dn_recv.at[k], z_dn)

    def hops(up, quarter):
        return 4 if up == (quarter % 2 == 0) else 3

    def y_copy(quarter):
        return remote(
            y_out.at[quarter], y_in.at[quarter], y_send.at[quarter], y_recv.at[quarter], partner
        )

    def ring_step(up, t, quarter):
        n = hops(up, quarter)
        if t >= n:
            return
        out, got = (up_out, up_in) if up else (dn_out, dn_in)
        val = partial(lax.rem(mz + NZ + (n - t if up else t - n), NZ), quarter)
        if t > 0:
            ring_copy(up, t - 1, quarter).wait_recv()
            val = val + got[4 * quarter + t - 1].astype(F32)
        out[4 * quarter + t] = val.astype(BF16)
        ring_copy(up, t, quarter).start()

    def ring_end(quarter):
        val = partial(mz, quarter)
        for up in (True, False):
            n = hops(up, quarter)
            ring_copy(up, n - 1, quarter).wait_recv()
            val = val + (up_in if up else dn_in)[4 * quarter + n - 1].astype(F32)
        summed[quarter] = val.reshape(2, NX * 16, OB)
        y_out[quarter] = summed[quarter, 1 - d0].astype(BF16)
        y_copy(quarter).start()

    def o_copies(quarter):
        made = []
        for i, where in enumerate(x_peers):
            if quarter == 0:
                src, dst = toto.at[where["dp_1"]], outo_ref.at[:, lanes(mx * OB, OB)]
            else:
                src = totq.at[quarter - 1, where["dp_1"]]
                dst = outq_ref.at[:, lanes(mx * QB + (quarter - 1) * OB, OB)]
            made.append(remote(src, dst, o_send.at[quarter, i], o_recv.at[quarter, i], where))
        return made

    def y_end(quarter, acc):
        y_copy(quarter).wait_recv()
        full = summed[quarter, d0] + y_in[quarter].astype(F32)
        by_x = full.reshape(NX, 16, OB)
        if quarter == 0:
            toto[...] = by_x
        else:
            totq[quarter - 1] = by_x
        for copy in o_copies(quarter):
            copy.start()
        full = full * full
        for c in range(2):
            for i in range(NX * 2):
                acc = acc + full[i * 8 : (i + 1) * 8, c * 128 : (c + 1) * 128]
        return acc

    acc = jnp.zeros((8, 128), F32)
    for wave in range(9):
        for quarter in range(4):
            t = wave - quarter
            if t == 0:
                exchanged(quarter)
            if 0 <= t < 4:
                for up in (True, False):
                    ring_step(up, t, quarter)
            if t == 4:
                ring_end(quarter)
            if t == 5:
                acc = y_end(quarter, acc)
    sqs[0] = acc

    def sum_over(peers, src, buf, ssem, rsem):
        copies = [
            remote(src, buf.at[i], ssem.at[i], rsem.at[i], where) for i, where in enumerate(peers)
        ]
        for copy in copies:
            copy.start()
        return copies

    def take(copies, src, buf):
        for copy in copies:
            copy.wait_recv()
        acc = src[...]
        for i in range(len(copies)):
            acc = acc + buf[i]
        return acc

    qz = sum_over(z_peers, sqs.at[0], sqz, qz_send, qz_recv)
    outo_ref[:, lanes(mx * OB, OB)] = toto[mx]
    for quarter in range(1, 4):
        outq_ref[:, lanes(mx * QB + (quarter - 1) * OB, OB)] = totq[quarter - 1, mx]
    sqs[1] = take(qz, sqs.at[0], sqz)
    qx = sum_over(x_peers, sqs.at[1], sqx, qx_send, qx_recv)
    sqs[2] = take(qx, sqs.at[1], sqx)
    qr = sum_over(r_peers, sqs.at[2], sqr, qr_send, qr_recv)
    total = take(qr, sqs.at[2], sqr)
    total = jnp.sum(jnp.sum(total, axis=1, keepdims=True), axis=0, keepdims=True)
    factor_ref[...] = jnp.broadcast_to(lax.rsqrt(total / 16777216.0 + 1e-12), (8, 128))
    for quarter in range(4):
        for copy in o_copies(quarter):
            copy.wait_recv()
    for quarter in range(4):
        for up in (True, False):
            for t in range(hops(up, quarter)):
                ring_copy(up, t, quarter).wait_send()
        y_copy(quarter).wait_send()
        for copy in o_copies(quarter):
            copy.wait_send()
    for copy in qz + qx + qr:
        copy.wait_send()

    def finish(m, carry):
        for copy in act_copies(m) + relays(m):
            copy.wait_send()
        for k in (2, 3, 4, 5):
            for copy in cot_copies(m, k):
                copy.wait_send()

        @pl.when(sec < 3)
        def _():
            h_copy(m, 0).wait_send()
            h_copy(m, 1).wait_send()

        @pl.when(sec > 0)
        def _():
            g_copy(m).wait_send()

        return carry

    lax.fori_loop(0, 2, finish, 0)

    @pl.when(s0 == 1)
    def _():
        swap_mod().wait_send()
        swap_noise().wait_send()


def run_step(h0, mod, noise, w_qkv, w_out, head):
    shape = jax.ShapeDtypeStruct
    dma = pltpu.SemaphoreType.DMA
    vmem = pltpu.VMEM
    rows = NX * 2 * SEQ
    return pl.pallas_call(
        step_kernel,
        out_shape=(shape((16, 3 * D), F32), shape((16, D), F32), shape((8, 128), F32)),
        in_specs=[VMEM, VMEM, VMEM, ANY, ANY, VMEM],
        out_specs=[VMEM] * 3,
        scratch_shapes=[
            vmem((D, 3 * D), BF16),
            vmem((D, D), BF16),
            vmem((3 * D, D), BF16),
            vmem((D, D), BF16),
            vmem((rows, D), BF16),
            vmem((rows, D), BF16),
            vmem((rows, QB), BF16),
            vmem((rows, OB), BF16),
            vmem((8, NZ, 16, rows), BF16),
            vmem((8, NZ, 16, rows), BF16),
            vmem((2, SEQ, D), BF16),
            vmem((2, SEQ, D), BF16),
            vmem((2, SEQ, D), BF16),
            vmem((2, SEQ, D), BF16),
            vmem((2, SEQ, 3 * D), BF16),
            vmem((2, HEADS // 2, 2 * SEQ, SEQ), F32),
            vmem((2, SEQ, 128), F32),
            vmem((2, SEQ, D), BF16),
            vmem((2, SEQ, D), BF16),
            vmem((2, SEQ, 3 * D), BF16),
            vmem((2, SEQ, D), BF16),
            vmem((SEQ, D), BF16),
            vmem((SEQ, D), BF16),
            vmem((8, 3 * D), F32),
            vmem((2, 16, SEQ), F32),
            vmem((16, 128, OB), BF16),
            vmem((16, 128, OB), BF16),
            vmem((16, 128, OB), BF16),
            vmem((16, 128, OB), BF16),
            vmem((4, 2, NX * 16, OB), F32),
            vmem((4, NX * 16, OB), BF16),
            vmem((4, NX * 16, OB), BF16),
            vmem((3, NX, 16, OB), F32),
            vmem((NX, 16, OB), F32),
            vmem((3, 8, 128), F32),
            vmem((NZ - 1, 8, 128), F32),
            vmem((NX - 1, 8, 128), F32),
            vmem((7, 8, 128), F32),
            dma((2, 2)), dma((2, 2)), dma((2,)), dma((2,)), dma((2,)), dma((2,)),
            dma((2, NX - 1, 6)), dma((2, NX - 1, 6)),
            dma((16,)), dma((16,)), dma((16,)), dma((16,)), dma((4,)), dma((4,)),
            dma((4, NX - 1)), dma((4, NX - 1)),
            dma((NZ - 1,)), dma((NZ - 1,)), dma((NX - 1,)), dma((NX - 1,)), dma((7,)), dma((7,)),
            dma((2,)),
        ],
        compiler_params=pltpu.CompilerParams(
            collective_id=0, has_side_effects=True, vmem_limit_bytes=58 * 2**20
        ),
        name="step",
    )(h0, mod, noise, w_qkv, w_out, head)


def optimizer_kernel(gq, go, factor_ref, mq, mo, vq, vo, uq, uo, nmq, nmo, nvq, nvo):
    factor = factor_ref[0:1, 0:1]
    for g, m, v, u, nm, nv in ((gq, mq, vq, uq, nmq, nvq), (go, mo, vo, uo, nmo, nvo)):
        normalized = g[...] * factor
        moment = 0.9 * m[0] + 0.1 * normalized
        second = 0.99 * v[0] + 0.01 * normalized * normalized
        u[0] = moment / (jnp.sqrt(second) + 1e-08)
        nm[0] = moment
        nv[0] = second


def optimizer(gq, go, factor, mq, mo, vq, vo):
    shape = jax.ShapeDtypeStruct
    big, small = shape((1, 16, 3 * D), F32), shape((1, 16, D), F32)
    return pl.pallas_call(
        optimizer_kernel,
        out_shape=(big, small, big, small, big, small),
        in_specs=[VMEM] * 7,
        out_specs=[VMEM] * 6,
        name="optimizer",
    )(gq, go, factor, mq, mo, vq, vo)


def local(
    latents,
    noise,
    timesteps,
    cameras,
    embed_in,
    camera_table,
    w_mod,
    w_qkv,
    w_out,
    head_out,
    moment_qkv,
    moment_out,
    second_qkv,
    second_out,
):
    time_emb = time_embed(timesteps, w_mod.shape[1])
    time_rows = jnp.pad(time_emb, ((0, 6), (0, 0)))
    mod = jnp.dot(time_rows, w_mod[0], preferred_element_type=jnp.float32)
    h0 = jax.vmap(embed_sample, in_axes=(0, 0, 0, 0, None, None))(
        latents, noise, timesteps, cameras, embed_in, camera_table
    )
    noise_rows = jnp.pad(noise.astype(F32), ((0, 0), (0, 12), (0, 0)))
    head = jnp.pad(head_out, ((0, 12), (0, 0)))
    qkv_rows, out_rows, factors = run_step(h0, mod, noise_rows, w_qkv[0], w_out[0], head)
    return optimizer(
        qkv_rows, out_rows, factors, moment_qkv, moment_out, second_qkv, second_out
    )


def solution(mesh):
    torus = Mesh(
        mesh.devices.reshape(2, 2, 2, 4, 8), ("section_0", "section_1", "dp_0", "dp_1", "dp_2")
    )
    return jax.shard_map(
        local,
        mesh=torus,
        in_specs=(
            P(DP, None, None),
            P(DP, None, None),
            P(DP),
            P(DP, None),
            P(),
            P(),
            P(SECTION, None, None),
            P(SECTION, None, None),
            P(SECTION, None, None),
            P(),
            P(SECTION, DP, None),
            P(SECTION, DP, None),
            P(SECTION, DP, None),
            P(SECTION, DP, None),
        ),
        out_specs=(
            P(SECTION, DP, None),
            P(SECTION, DP, None),
            P(SECTION, DP, None),
            P(SECTION, DP, None),
            P(SECTION, DP, None),
            P(SECTION, DP, None),
        ),
        check_vma=False,
    )
```

time: 190 us -> 140 us (0.74)
  Pallas kernels: 169 us -> 130 us
  local copies, waits for them, and re-layouts: 5.92 us -> 1.37 us
  other arithmetic: 4.5 us -> 0.97 us
  matrix products: 6.89 us -> 3.97 us
    pallas_call x2, Pallas kernels: 169 us -> 130 us  [the longest x1 128 us: run_step(): pl.pallas_call(step_kernel, out_shape=(shape((16, 3 * D), F32), shape((16...]
    dot_general x3 -> x1, matrix products: 4.87 us -> 0.96 us  [local(): mod = jnp.dot(time_rows, w_mod[0], preferred_element_type=jnp.float32)]
    concatenate x1 -> x0, local copies, waits for them, and re-layouts: 2.85 us -> none  [local(): jnp.concatenate([dot_tn(nall.reshape(rows, D), ball.reshape(rows, QB)).as...]
    unnamed x20 -> x8, local copies, waits for them, and re-layouts: 2.63 us -> 0.03 us
where the time goes in v2:
time: 140 us; the launch traced here: 137 us
  Pallas kernels  130 us (93%)
  matrix products  3.97 us (3%)
    pallas_call x1, Pallas kernels, run_step(): pl.pallas_call(step_kernel, out_shape=(shape((16, 3 * D), F32), shape((16...  128 us

profile of v2, /device:TPU:8, one launch (start us, length us, event | category | flops | bytes accessed | tf_op | source)
XLA Modules:
  0.0 137.3 jit_solution(14263941508559062670)
XLA Ops:
  0.6 0.0 copy-start
  0.6 0.0 copy-start.3
  0.7 0.8 fusion.13
  1.5 1.1 fusion.3
  2.5 0.1 add.29
  2.7 0.0 copy-start.2
  2.7 0.0 copy-start.1
  2.7 2.0 %fusion.2.h0_ref = bf16[2,128,1024]{2,1,0:T(8,128)(2,1)} fusion(f32[2,128,1024]{2,1,0:T(8,128)S(1)} %bitcast.13, bf16[4,1024]{1,0:T(4,128)(2,1)} %param.18, bf16[2,4,128]{2,1,0:T(4,128)(2,1)} %param.14, f32[2]{0:T(128)S(1)} %get-tuple-element.15, f32[2]{0:T(128)S(1)} %get-tuple-element.14, bf16[2,4,128]{2,1,0:T(4,128)(2,1)} %param.15), kind=kOutput, calls=%fused_computation.3 | convolution fusion | flops 2627584 | bytes 1585168 | tf_op jit(solution)/shard_map/vmap()/dot_general | solution.py:43
  4.6 0.0 copy-done.3
  4.7 0.1 multiply_cosine_fusion
  4.8 0.0 copy-done
  4.8 1.0 fusion.mod_ref
  5.8 0.0 copy-done.2
  5.8 0.6 pad.14.head_ref
  6.4 0.0 copy-done.1
  6.4 0.6 pad.13.noise_ref
  7.0 128.2 %step.1 = (f32[16,3072]{1,0:T(8,128)}, f32[16,1024]{1,0:T(8,128)}, f32[8,128]{1,0:T(8,128)}) custom-call(bf16[2,128,1024]{2,1,0:T(8,128)(2,1)} %fusion.2.h0_ref, f32[8,3072]{1,0:T(8,128)} %fusion.mod_ref, f32[2,16,128]{2,1,0:T(8,128)} %pad.13.noise_ref, bf16[1024,3072]{1,0:T(8,128)(2,1)} %bitcast.12, bf16[1024,1024]{1,0:T(8,128)(2,1)} %bitcast.14, ...), custom_call_target="tpu_custom_call" | custom-call | tf_op jit(solution)/shard_map/step/pallas_call | solution.py:578
  135.2 2.1 %optimizer.1 = (f32[1,16,3072]{2,1,0:T(8,128)}, f32[1,16,1024]{2,1,0:T(8,128)}, f32[1,16,3072]{2,1,0:T(8,128)}, f32[1,16,1024]{2,1,0:T(8,128)}, f32[1,16,3072]{2,1,0:T(8,128)}, /*index=5*/f32[1,16,1024]{2,1,0:T(8,128)}) custom-call(f32[16,3072]{1,0:T(8,128)} %get-tuple-element.9.gq, f32[16,1024]{1,0:T(8,128)} %get-tuple-element.10.go, ...), custom_call_target="tpu_custom_call" | custom-call | tf_op jit(solution)/shard_map/optimizer/pallas_call | solution.py:650
  (3 shorter events, 0.0 us)
Async XLA Ops:
  0.6 4.2 %copy-start = (bf16[1,256,3072]{2,1,0:T(8,128)(2,1)S(1)}, bf16[1,256,3072]{2,1,0:T(8,128)(2,1)}, u32[]{:S(2)}) copy-start(bf16[1,256,3072]{2,1,0:T(8,128)(2,1)} %param.20) | copy-start | bytes 4718596
  0.6 4.0 %copy-start.3 = (s32[2]{0:T(128)S(1)}, s32[2]{0:T(128)}, u32[]{:S(2)}) copy-start(s32[2]{0:T(128)} %param.16) | copy-start | bytes 28
  2.7 3.1 %copy-start.2 = (bf16[4,1024]{1,0:T(4,128)(2,1)S(1)}, bf16[4,1024]{1,0:T(4,128)(2,1)}, u32[]{:S(2)}) copy-start(bf16[4,1024]{1,0:T(4,128)(2,1)} %param.23) | copy-start | bytes 24580
  2.7 3.7 %copy-start.1 = (bf16[2,4,128]{2,1,0:T(4,128)(2,1)S(1)}, bf16[2,4,128]{2,1,0:T(4,128)(2,1)}, u32[]{:S(2)}) copy-start(bf16[2,4,128]{2,1,0:T(4,128)(2,1)} %param.15) | copy-start | bytes 6148

commit v3 on v2

--- a/solution.py
+++ b/solution.py
@@ -78,9 +78,9 @@
     wqkv_ref, wout_ref, wqkv_t, wout_t, nall, aall, ball, pall, n_t, a_t,
     h_scr, hn_scr, nrm_scr, att_scr, qkv_scr, p_scr, r_scr, g_scr, gs_scr,
     dqkv_scr, pc_scr, datt_scr, tmp_scr, mods, noi,
-    up_out, up_in, dn_out, dn_in, summed, y_out, y_in, totq, toto, sqs, sqz, sqx, sqr,
+    up_out, up_in, dn_out, dn_in, c_sum, c_out, c_in, summed, y_out, y_in, totq, toto, sqs, sqz, sqx, sqr,
     h_send, h_recv, g_send, g_recv, sw_send, sw_recv, x_send, x_recv,
-    up_send, up_recv, dn_send, dn_recv, y_send, y_recv, o_send, o_recv,
+    up_send, up_recv, dn_send, dn_recv, c_send, c_recv, y_send, y_recv, o_send, o_recv,
     qz_send, qz_recv, qx_send, qx_recv, qr_send, qr_recv, w_sem,
 ):
     w_copies = [
@@ -183,31 +183,23 @@
         )
         return remote(src, dst, x_send.at[m, d - 1, k], x_recv.at[m, d - 1, k], {"dp_1": to})
 
-    def act_copies(m):
-        return [x_copy(m, d, k) for k in (0, 1) for d in (1, 3)]
+    def act_copies(m, k):
+        return [x_copy(m, d, k) for d in (1, 3)]
 
     def cot_copies(m, k):
         return [x_copy(m, d, k) for d in (1, 2, 3)]
 
-    def relays(m):
-        left, right = lax.rem(mx + 3, NX), lax.rem(mx + 1, NX)
-        nrows, arows = rows_of(left, m), rows_of(right, m)
-        return [
-            remote(
-                nall.at[nrows], nall.at[nrows], x_send.at[m, 1, 0], x_recv.at[m, 1, 0],
-                {"dp_1": right},
-            ),
-            remote(
-                aall.at[arows], aall.at[arows], x_send.at[m, 1, 1], x_recv.at[m, 1, 1],
-                {"dp_1": left},
-            ),
-        ]
-
-    def relay(m):
-        x_copy(m, 1, 0).wait_recv()
-        x_copy(m, 3, 1).wait_recv()
-        for copy in relays(m):
-            copy.start()
+    def relay_copy(m, k):
+        by = 1 if k == 0 else 3
+        rows = rows_of(lax.rem(mx + NX - by, NX), m)
+        held = (nall, aall)[k].at[rows]
+        return remote(
+            held, held, x_send.at[m, 1, k], x_recv.at[m, 1, k], {"dp_1": lax.rem(mx + by, NX)}
+        )
+
+    def relay(m, k):
+        x_copy(m, 1 if k == 0 else 3, k).wait_recv()
+        relay_copy(m, k).start()
 
     low = lax.broadcasted_iota(jnp.int32, (SEQ, 128), 1) < HEAD_DIM
 
@@ -272,11 +264,16 @@
             def _():
                 h_copy(m, n).start()
 
-        for copy in act_copies(m):
+        for copy in act_copies(m, 0):
             copy.start()
         rows = rows_of(mx, m)
         nall[rows] = nrm_scr[m]
-        aall[rows] = att_scr[m]
+
+        @pl.when(s0 == 0)
+        def _():
+            for copy in act_copies(m, 1):
+                copy.start()
+            aall[rows] = att_scr[m]
 
         @pl.when(sec == 3)
         def _():
@@ -311,35 +308,36 @@
 
     lax.fori_loop(0, 2, forward, 0)
 
-    def turn():
+    def turn(k):
         def arrived(m, carry):
-            x_copy(m, 3, 0).wait_recv()
-            x_copy(m, 1, 1).wait_recv()
-            for copy in relays(m):
-                copy.wait_recv()
+            x_copy(m, 3 if k == 0 else 1, k).wait_recv()
+            relay_copy(m, k).wait_recv()
             return carry
 
         lax.fori_loop(0, 2, arrived, 0)
 
         def block(i, carry):
             here = lanes(i * SEQ, SEQ)
-            for src, dst in ((nall, n_t), (aall, a_t)):
-                for g in range(8):
-                    tile = src[here, pl.ds(g * 128, 128)]
-                    dst[g, :, :, here] = jnp.transpose(tile).reshape(NZ, 16, SEQ)
+            src, dst = ((nall, n_t), (aall, a_t))[k]
+            for g in range(8):
+                tile = src[here, pl.ds(g * 128, 128)]
+                dst[g, :, :, here] = jnp.transpose(tile).reshape(NZ, 16, SEQ)
             return carry
 
         lax.fori_loop(0, 2 * NX, block, 0)
 
     @pl.when(sec < 3)
     def _():
-        relay(0)
+        relay(0, 0)
 
     @pl.when(s0 == 0)
     def _():
-        relay(1)
+        relay(1, 0)
+        relay(0, 1)
+        relay(1, 1)
         turn_weights()
-        turn()
+        turn(0)
+        turn(1)
 
     def backward(m, carry):
         @pl.when(sec < 3)
@@ -349,8 +347,12 @@
         scale = mods[pl.ds(m, 1), pl.ds(D, D)]
         gate = mods[pl.ds(m, 1), pl.ds(2 * D, D)]
         pc_scr[m] = (gate * g_scr[m].astype(F32)).astype(BF16)
-        for copy in cot_copies(m, 2):
-            copy.start()
+
+        @pl.when(s0 == 0)
+        def _():
+            for copy in cot_copies(m, 2):
+                copy.start()
+
         for n in range(2):
             cols = pl.ds(n * 512, 512)
             datt_scr[:, cols] = dot_nn(pc_scr[m], wout_t[:, cols]).astype(BF16)
@@ -394,7 +396,7 @@
 
         @pl.when((sec == 2) & (m == 0))
         def _():
-            relay(1)
+            relay(1, 0)
 
         return carry
 
@@ -402,12 +404,8 @@
 
     @pl.when(sec == 3)
     def _():
-        relay(0)
-        relay(1)
-
-    @pl.when(s0 == 1)
-    def _():
-        turn()
+        relay(0, 0)
+        relay(1, 0)
 
     def exchanged(quarter):
         def arrive(m, carry):
@@ -417,11 +415,24 @@
 
         lax.fori_loop(0, 2, arrive, 0)
 
-    def partial(dest, quarter):
-        left = (n_t if quarter else a_t)[:, dest].reshape(8 * 16, NX * 2 * SEQ)
-        if quarter == 0:
-            return dot_nn(left, pall[...])
-        return dot_nn(left, ball[:, pl.ds((quarter - 1) * OB, OB)])
+    def partial(quarter):
+        def of(dest):
+            left = (n_t if quarter else a_t)[:, dest].reshape(8 * 16, NX * 2 * SEQ)
+            if quarter == 0:
+                return dot_nn(left, pall[...])
+            return dot_nn(left, ball[:, pl.ds((quarter - 1) * OB, OB)])
+
+        return of
+
+    def wide(c):
+        def of(dest):
+            left = a_t[:, dest, :, pl.ds(0, 2 * SEQ)].reshape(8 * 16, 2 * SEQ)
+            return dot_nn(left, pc_scr[:, :, pl.ds(c * OB, OB)].reshape(2 * SEQ, OB))
+
+        return of
+
+    def wide_ring(c):
+        return 3 + c if c else 0
 
     z_up = {"dp_2": lax.rem(mz + 1, NZ)}
     z_dn = {"dp_2": lax.rem(mz + NZ - 1, NZ)}
@@ -440,27 +451,37 @@
             y_out.at[quarter], y_in.at[quarter], y_send.at[quarter], y_recv.at[quarter], partner
         )
 
-    def ring_step(up, t, quarter):
-        n = hops(up, quarter)
-        if t >= n:
-            return
-        out, got = (up_out, up_in) if up else (dn_out, dn_in)
-        val = partial(lax.rem(mz + NZ + (n - t if up else t - n), NZ), quarter)
-        if t > 0:
-            ring_copy(up, t - 1, quarter).wait_recv()
-            val = val + got[4 * quarter + t - 1].astype(F32)
-        out[4 * quarter + t] = val.astype(BF16)
-        ring_copy(up, t, quarter).start()
-
-    def ring_end(quarter):
-        val = partial(mz, quarter)
+    def ring_step(t, ring, part):
         for up in (True, False):
-            n = hops(up, quarter)
-            ring_copy(up, n - 1, quarter).wait_recv()
-            val = val + (up_in if up else dn_in)[4 * quarter + n - 1].astype(F32)
+            n = hops(up, ring)
+            if t >= n:
+                continue
+            out, got = (up_out, up_in) if up else (dn_out, dn_in)
+            val = part(lax.rem(mz + NZ + (n - t if up else t - n), NZ))
+            if t > 0:
+                ring_copy(up, t - 1, ring).wait_recv()
+                val = val + got[4 * ring + t - 1].astype(F32)
+            out[4 * ring + t] = val.astype(BF16)
+            ring_copy(up, t, ring).start()
+
+    def ring_sum(ring, part):
+        val = part(mz)
+        for up in (True, False):
+            n = hops(up, ring)
+            ring_copy(up, n - 1, ring).wait_recv()
+            val = val + (up_in if up else dn_in)[4 * ring + n - 1].astype(F32)
+        return val
+
+    def ring_end(quarter, val):
         summed[quarter] = val.reshape(2, NX * 16, OB)
         y_out[quarter] = summed[quarter, 1 - d0].astype(BF16)
         y_copy(quarter).start()
+
+    def c_copy(d):
+        to = lax.rem(mx + d, NX)
+        return remote(
+            c_out.at[to], c_in.at[d - 1], c_send.at[d - 1], c_recv.at[d - 1], {"dp_1": to}
+        )
 
     def o_copies(quarter):
         made = []
@@ -489,19 +510,48 @@
                 acc = acc + full[i * 8 : (i + 1) * 8, c * 128 : (c + 1) * 128]
         return acc
 
-    acc = jnp.zeros((8, 128), F32)
-    for wave in range(9):
-        for quarter in range(4):
-            t = wave - quarter
+    @pl.when(s0 == 0)
+    def _():
+        exchanged(0)
+        for t in range(4):
+            ring_step(t, 0, partial(0))
+        ring_end(0, ring_sum(0, partial(0)))
+
+    @pl.when(s0 == 1)
+    def _():
+        for m in range(2):
+            for g in range(8):
+                tile = att_scr[m, :, pl.ds(g * 128, 128)]
+                a_t[g, :, :, pl.ds(m * SEQ, SEQ)] = jnp.transpose(tile).reshape(NZ, 16, SEQ)
+        for t in range(4):
+            for c in range(NX):
+                ring_step(t, wide_ring(c), wide(c))
+        for c in range(NX):
+            c_sum[c] = ring_sum(wide_ring(c), wide(c))
+            c_out[c] = c_sum[c].astype(BF16)
+        for d in range(1, NX):
+            c_copy(d).start()
+        turn(0)
+
+    for t in range(4):
+        for quarter in range(1, 4):
             if t == 0:
                 exchanged(quarter)
-            if 0 <= t < 4:
-                for up in (True, False):
-                    ring_step(up, t, quarter)
-            if t == 4:
-                ring_end(quarter)
-            if t == 5:
-                acc = y_end(quarter, acc)
+            ring_step(t, quarter, partial(quarter))
+
+    @pl.when(s0 == 1)
+    def _():
+        val = c_sum[mx]
+        for d in range(1, NX):
+            c_copy(d).wait_recv()
+            val = val + c_in[d - 1].astype(F32)
+        ring_end(0, val)
+
+    for quarter in range(1, 4):
+        ring_end(quarter, ring_sum(quarter, partial(quarter)))
+    acc = jnp.zeros((8, 128), F32)
+    for quarter in range(4):
+        acc = y_end(quarter, acc)
     sqs[0] = acc
 
     def sum_over(peers, src, buf, ssem, rsem):
@@ -534,21 +584,36 @@
     for quarter in range(4):
         for copy in o_copies(quarter):
             copy.wait_recv()
+    def ring_sent(ring):
+        for up in (True, False):
+            for t in range(hops(up, ring)):
+                ring_copy(up, t, ring).wait_send()
+
     for quarter in range(4):
-        for up in (True, False):
-            for t in range(hops(up, quarter)):
-                ring_copy(up, t, quarter).wait_send()
+        ring_sent(quarter)
         y_copy(quarter).wait_send()
         for copy in o_copies(quarter):
             copy.wait_send()
+
+    @pl.when(s0 == 1)
+    def _():
+        for c in range(1, NX):
+            ring_sent(wide_ring(c))
+            c_copy(c).wait_send()
+
     for copy in qz + qx + qr:
         copy.wait_send()
 
     def finish(m, carry):
-        for copy in act_copies(m) + relays(m):
+        for copy in act_copies(m, 0) + [relay_copy(m, 0)]:
             copy.wait_send()
-        for k in (2, 3, 4, 5):
+        for k in (3, 4, 5):
             for copy in cot_copies(m, k):
+                copy.wait_send()
+
+        @pl.when(s0 == 0)
+        def _():
+            for copy in act_copies(m, 1) + [relay_copy(m, 1)] + cot_copies(m, 2):
                 copy.wait_send()
 
         @pl.when(sec < 3)
@@ -606,10 +671,13 @@
             vmem((SEQ, D), BF16),
             vmem((8, 3 * D), F32),
             vmem((2, 16, SEQ), F32),
-            vmem((16, 128, OB), BF16),
-            vmem((16, 128, OB), BF16),
-            vmem((16, 128, OB), BF16),
-            vmem((16, 128, OB), BF16),
+            vmem((28, 128, OB), BF16),
+            vmem((28, 128, OB), BF16),
+            vmem((28, 128, OB), BF16),
+            vmem((28, 128, OB), BF16),
+            vmem((NX, 128, OB), F32),
+            vmem((NX, 128, OB), BF16),
+            vmem((NX - 1, 128, OB), BF16),
             vmem((4, 2, NX * 16, OB), F32),
             vmem((4, NX * 16, OB), BF16),
             vmem((4, NX * 16, OB), BF16),
@@ -621,7 +689,8 @@
             vmem((7, 8, 128), F32),
             dma((2, 2)), dma((2, 2)), dma((2,)), dma((2,)), dma((2,)), dma((2,)),
             dma((2, NX - 1, 6)), dma((2, NX - 1, 6)),
-            dma((16,)), dma((16,)), dma((16,)), dma((16,)), dma((4,)), dma((4,)),
+            dma((28,)), dma((28,)), dma((28,)), dma((28,)), dma((NX - 1,)), dma((NX - 1,)),
+            dma((4,)), dma((4,)),
             dma((4, NX - 1)), dma((4, NX - 1)),
             dma((NZ - 1,)), dma((NZ - 1,)), dma((NX - 1,)), dma((NX - 1,)), dma((7,)), dma((7,)),
             dma((2,)),

time: 140 us -> 137 us (0.979)
    pallas_call x1, Pallas kernels: 128 us -> 126 us  [run_step(): pl.pallas_call(step_kernel, out_shape=(shape((16, 3 * D), F32), shape((16...]
where the time goes in v3:
time: 137 us; the launch traced here: 136 us
  Pallas kernels  129 us (94%)
  matrix products  3.97 us (3%)
  local copies, waits for them, and re-layouts  1.37 us (1%)
    pallas_call x1, Pallas kernels, run_step(): pl.pallas_call(step_kernel, out_shape=(shape((16, 3 * D), F32), shape((16...  126 us

profile of v3, /device:TPU:8, one launch (start us, length us, event | category | flops | bytes accessed | tf_op | source)
XLA Modules:
  0.0 135.6 jit_solution(10402558964282564748)
XLA Ops:
  0.6 0.0 copy-start
  0.6 0.0 copy-start.3
  0.7 0.8 fusion.13
  1.5 1.1 fusion.3
  2.5 0.1 add.29
  2.7 0.0 copy-start.2
  2.7 0.0 copy-start.1
  2.7 2.0 %fusion.2.h0_ref = bf16[2,128,1024]{2,1,0:T(8,128)(2,1)} fusion(f32[2,128,1024]{2,1,0:T(8,128)S(1)} %bitcast.13, bf16[4,1024]{1,0:T(4,128)(2,1)} %param.18, bf16[2,4,128]{2,1,0:T(4,128)(2,1)} %param.14, f32[2]{0:T(128)S(1)} %get-tuple-element.15, f32[2]{0:T(128)S(1)} %get-tuple-element.14, bf16[2,4,128]{2,1,0:T(4,128)(2,1)} %param.15), kind=kOutput, calls=%fused_computation.3 | convolution fusion | flops 2627584 | bytes 1585168 | tf_op jit(solution)/shard_map/vmap()/dot_general | solution.py:43
  4.6 0.0 copy-done.3
  4.7 0.1 multiply_cosine_fusion
  4.8 0.0 copy-done
  4.8 1.0 fusion.mod_ref
  5.8 0.0 copy-done.2
  5.8 0.6 pad.14.head_ref
  6.4 0.0 copy-done.1
  6.4 0.6 pad.13.noise_ref
  7.0 126.4 %step.1 = (f32[16,3072]{1,0:T(8,128)}, f32[16,1024]{1,0:T(8,128)}, f32[8,128]{1,0:T(8,128)}) custom-call(bf16[2,128,1024]{2,1,0:T(8,128)(2,1)} %fusion.2.h0_ref, f32[8,3072]{1,0:T(8,128)} %fusion.mod_ref, f32[2,16,128]{2,1,0:T(8,128)} %pad.13.noise_ref, bf16[1024,3072]{1,0:T(8,128)(2,1)} %bitcast.12, bf16[1024,1024]{1,0:T(8,128)(2,1)} %bitcast.14, ...), custom_call_target="tpu_custom_call" | custom-call | tf_op jit(solution)/shard_map/step/pallas_call | solution.py:643
  133.4 2.1 %optimizer.1 = (f32[1,16,3072]{2,1,0:T(8,128)}, f32[1,16,1024]{2,1,0:T(8,128)}, f32[1,16,3072]{2,1,0:T(8,128)}, f32[1,16,1024]{2,1,0:T(8,128)}, f32[1,16,3072]{2,1,0:T(8,128)}, /*index=5*/f32[1,16,1024]{2,1,0:T(8,128)}) custom-call(f32[16,3072]{1,0:T(8,128)} %get-tuple-element.9.gq, f32[16,1024]{1,0:T(8,128)} %get-tuple-element.10.go, ...), custom_call_target="tpu_custom_call" | custom-call | tf_op jit(solution)/shard_map/optimizer/pallas_call | solution.py:719
  (3 shorter events, 0.0 us)
Async XLA Ops:
  0.6 4.2 %copy-start = (bf16[1,256,3072]{2,1,0:T(8,128)(2,1)S(1)}, bf16[1,256,3072]{2,1,0:T(8,128)(2,1)}, u32[]{:S(2)}) copy-start(bf16[1,256,3072]{2,1,0:T(8,128)(2,1)} %param.20) | copy-start | bytes 4718596
  0.6 4.0 %copy-start.3 = (s32[2]{0:T(128)S(1)}, s32[2]{0:T(128)}, u32[]{:S(2)}) copy-start(s32[2]{0:T(128)} %param.16) | copy-start | bytes 28
  2.7 3.1 %copy-start.2 = (bf16[4,1024]{1,0:T(4,128)(2,1)S(1)}, bf16[4,1024]{1,0:T(4,128)(2,1)}, u32[]{:S(2)}) copy-start(bf16[4,1024]{1,0:T(4,128)(2,1)} %param.23) | copy-start | bytes 24580
  2.7 3.7 %copy-start.1 = (bf16[2,4,128]{2,1,0:T(4,128)(2,1)S(1)}, bf16[2,4,128]{2,1,0:T(4,128)(2,1)}, u32[]{:S(2)}) copy-start(bf16[2,4,128]{2,1,0:T(4,128)(2,1)} %param.15) | copy-start | bytes 6148

commit v4 on v3

--- a/solution.py
+++ b/solution.py
@@ -78,10 +78,10 @@
     wqkv_ref, wout_ref, wqkv_t, wout_t, nall, aall, ball, pall, n_t, a_t,
     h_scr, hn_scr, nrm_scr, att_scr, qkv_scr, p_scr, r_scr, g_scr, gs_scr,
     dqkv_scr, pc_scr, datt_scr, tmp_scr, mods, noi,
-    up_out, up_in, dn_out, dn_in, c_sum, c_out, c_in, summed, y_out, y_in, totq, toto, sqs, sqz, sqx, sqr,
+    up_out, up_in, dn_out, dn_in, c_sum, c_out, c_in, share, summed, y_out, y_in, totq, toto, sqs, sqz, sqp,
     h_send, h_recv, g_send, g_recv, sw_send, sw_recv, x_send, x_recv,
     up_send, up_recv, dn_send, dn_recv, c_send, c_recv, y_send, y_recv, o_send, o_recv,
-    qz_send, qz_recv, qx_send, qx_recv, qr_send, qr_recv, w_sem,
+    qz_send, qz_recv, qp_send, qp_recv, w_sem,
 ):
     w_copies = [
         pltpu.make_async_copy(wqkv_hbm, wqkv_ref, w_sem.at[0]),
@@ -118,11 +118,16 @@
 
     z_peers = [{"dp_2": lax.rem(mz + d, NZ)} for d in range(1, NZ)]
     x_peers = [{"dp_1": lax.rem(mx + d, NX)} for d in range(1, NX)]
-    r_peers = [
-        {"section_0": flip(s0, c & 4), "section_1": flip(s1, c & 2), "dp_0": flip(d0, c & 1)}
-        for c in range(1, 8)
+    plane = [
+        {
+            "section_0": flip(s0, c & 4),
+            "section_1": flip(s1, c & 2),
+            "dp_0": flip(d0, c & 1),
+            "dp_1": lax.rem(mx + c // 8, NX),
+        }
+        for c in range(1, 32)
     ]
-    for where in z_peers + x_peers + r_peers:
+    for where in z_peers + plane:
         greet(where)
 
     @pl.when(sec < 3)
@@ -133,7 +138,7 @@
     def _():
         greet(prv)
 
-    pl.semaphore_wait(barrier, 17 + lax.min(sec, 1) + lax.min(3 - sec, 1))
+    pl.semaphore_wait(barrier, 38 + lax.min(sec, 1) + lax.min(3 - sec, 1))
 
     def remote(src, dst, ssem, rsem, where):
         return pltpu.make_async_remote_copy(
@@ -211,7 +216,7 @@
         return jnp.where(low, pair[:SEQ], pair[SEQ:])
 
     PAIRS = HEADS // 2
-    GROUP = 4
+    GROUP = 8
 
     def over_pairs(body):
         def step(i, carry):
@@ -269,7 +274,7 @@
         rows = rows_of(mx, m)
         nall[rows] = nrm_scr[m]
 
-        @pl.when(s0 == 0)
+        @pl.when(sec == 4)
         def _():
             for copy in act_copies(m, 1):
                 copy.start()
@@ -280,7 +285,7 @@
             ff = hn_scr[m].astype(F32)
             rr = lax.rsqrt(jnp.mean(ff * ff, axis=-1, keepdims=True) + 1e-06)
             predicted = dot_nt(head_ref[...], (ff * rr).astype(BF16))
-            err = 2.0 * (predicted - noi[m])
+            err = 2.0 * (predicted - noi[m].astype(F32))
             hi = err.astype(BF16)
             lo = (err - hi.astype(F32)).astype(BF16)
             dn = (dot_tn(hi, head_ref[...]) + dot_tn(lo, head_ref[...])).astype(BF16).astype(F32)
@@ -333,10 +338,13 @@
     @pl.when(s0 == 0)
     def _():
         relay(1, 0)
+        turn_weights()
+        turn(0)
+
+    @pl.when(sec == 4)
+    def _():
         relay(0, 1)
         relay(1, 1)
-        turn_weights()
-        turn(0)
         turn(1)
 
     def backward(m, carry):
@@ -348,7 +356,7 @@
         gate = mods[pl.ds(m, 1), pl.ds(2 * D, D)]
         pc_scr[m] = (gate * g_scr[m].astype(F32)).astype(BF16)
 
-        @pl.when(s0 == 0)
+        @pl.when(sec == 4)
         def _():
             for copy in cot_copies(m, 2):
                 copy.start()
@@ -415,21 +423,36 @@
 
         lax.fori_loop(0, 2, arrive, 0)
 
-    def partial(quarter):
-        def of(dest):
-            left = (n_t if quarter else a_t)[:, dest].reshape(8 * 16, NX * 2 * SEQ)
-            if quarter == 0:
-                return dot_nn(left, pall[...])
-            return dot_nn(left, ball[:, pl.ds((quarter - 1) * OB, OB)])
-
-        return of
-
-    def wide(c):
-        def of(dest):
-            left = a_t[:, dest, :, pl.ds(0, 2 * SEQ)].reshape(8 * 16, 2 * SEQ)
-            return dot_nn(left, pc_scr[:, :, pl.ds(c * OB, OB)].reshape(2 * SEQ, OB))
-
-        return of
+    def multiply(ring, left_of, right_of):
+        def rows(i, carry):
+            val = dot_nn(left_of(i), right_of())
+            share[ring, pl.ds(2 * i, 2)] = val.reshape(2, NZ, 16, OB)
+            return carry
+
+        lax.fori_loop(0, 4, rows, 0)
+
+    def multiply_all(quarter):
+        src = n_t if quarter else a_t
+
+        def left(i):
+            return src[pl.ds(2 * i, 2)].reshape(256, NX * 2 * SEQ)
+
+        def right():
+            return ball[:, pl.ds((quarter - 1) * OB, OB)] if quarter else pall[...]
+
+        multiply(quarter, left, right)
+
+    def multiply_own(c):
+        def left(i):
+            return a_t[pl.ds(2 * i, 2), :, :, pl.ds(0, 2 * SEQ)].reshape(256, 2 * SEQ)
+
+        def right():
+            return pc_scr[:, :, pl.ds(c * OB, OB)].reshape(2 * SEQ, OB)
+
+        multiply(wide_ring(c), left, right)
+
+    def part(ring, dest):
+        return share[ring, :, dest].reshape(128, OB)
 
     def wide_ring(c):
         return 3 + c if c else 0
@@ -451,21 +474,21 @@
             y_out.at[quarter], y_in.at[quarter], y_send.at[quarter], y_recv.at[quarter], partner
         )
 
-    def ring_step(t, ring, part):
+    def ring_step(t, ring):
         for up in (True, False):
             n = hops(up, ring)
             if t >= n:
                 continue
             out, got = (up_out, up_in) if up else (dn_out, dn_in)
-            val = part(lax.rem(mz + NZ + (n - t if up else t - n), NZ))
+            val = part(ring, lax.rem(mz + NZ + (n - t if up else t - n), NZ))
             if t > 0:
                 ring_copy(up, t - 1, ring).wait_recv()
                 val = val + got[4 * ring + t - 1].astype(F32)
             out[4 * ring + t] = val.astype(BF16)
             ring_copy(up, t, ring).start()
 
-    def ring_sum(ring, part):
-        val = part(mz)
+    def ring_sum(ring):
+        val = part(ring, mz)
         for up in (True, False):
             n = hops(up, ring)
             ring_copy(up, n - 1, ring).wait_recv()
@@ -510,36 +533,69 @@
                 acc = acc + full[i * 8 : (i + 1) * 8, c * 128 : (c + 1) * 128]
         return acc
 
-    @pl.when(s0 == 0)
-    def _():
-        exchanged(0)
-        for t in range(4):
-            ring_step(t, 0, partial(0))
-        ring_end(0, ring_sum(0, partial(0)))
-
-    @pl.when(s0 == 1)
-    def _():
+    def own_shares():
         for m in range(2):
             for g in range(8):
                 tile = att_scr[m, :, pl.ds(g * 128, 128)]
                 a_t[g, :, :, pl.ds(m * SEQ, SEQ)] = jnp.transpose(tile).reshape(NZ, 16, SEQ)
-        for t in range(4):
-            for c in range(NX):
-                ring_step(t, wide_ring(c), wide(c))
         for c in range(NX):
-            c_sum[c] = ring_sum(wide_ring(c), wide(c))
+            multiply_own(c)
+            ring_step(0, wide_ring(c))
+
+    def own_steps(t):
+        for c in range(NX):
+            ring_step(t, wide_ring(c))
+
+    def own_sums():
+        for c in range(NX):
+            c_sum[c] = ring_sum(wide_ring(c))
             c_out[c] = c_sum[c].astype(BF16)
         for d in range(1, NX):
             c_copy(d).start()
+
+    @pl.when(sec == 4)
+    def _():
+        exchanged(0)
+        multiply_all(0)
+        ring_step(0, 0)
+
+    own_shares()
+
+    @pl.when(s0 == 1)
+    def _():
+        for t in range(1, 4):
+            own_steps(t)
+        own_sums()
         turn(0)
 
-    for t in range(4):
+    for quarter in range(1, 4):
+        exchanged(quarter)
+        multiply_all(quarter)
+        ring_step(0, quarter)
+    for t in range(1, 4):
+        @pl.when(sec == 4)
+        def _():
+            ring_step(t, 0)
+
+        @pl.when(s0 == 0)
+        def _():
+            own_steps(t)
+
         for quarter in range(1, 4):
-            if t == 0:
-                exchanged(quarter)
-            ring_step(t, quarter, partial(quarter))
-
-    @pl.when(s0 == 1)
+            ring_step(t, quarter)
+
+    @pl.when(sec == 4)
+    def _():
+        ring_end(0, ring_sum(0))
+
+    @pl.when(s0 == 0)
+    def _():
+        own_sums()
+
+    for quarter in range(1, 4):
+        ring_end(quarter, ring_sum(quarter))
+
+    @pl.when(sec < 4)
     def _():
         val = c_sum[mx]
         for d in range(1, NX):
@@ -547,10 +603,8 @@
             val = val + c_in[d - 1].astype(F32)
         ring_end(0, val)
 
-    for quarter in range(1, 4):
-        ring_end(quarter, ring_sum(quarter, partial(quarter)))
     acc = jnp.zeros((8, 128), F32)
-    for quarter in range(4):
+    for quarter in (1, 2, 3, 0):
         acc = y_end(quarter, acc)
     sqs[0] = acc
 
@@ -575,10 +629,8 @@
     for quarter in range(1, 4):
         outq_ref[:, lanes(mx * QB + (quarter - 1) * OB, OB)] = totq[quarter - 1, mx]
     sqs[1] = take(qz, sqs.at[0], sqz)
-    qx = sum_over(x_peers, sqs.at[1], sqx, qx_send, qx_recv)
-    sqs[2] = take(qx, sqs.at[1], sqx)
-    qr = sum_over(r_peers, sqs.at[2], sqr, qr_send, qr_recv)
-    total = take(qr, sqs.at[2], sqr)
+    qp = sum_over(plane, sqs.at[1], sqp, qp_send, qp_recv)
+    total = take(qp, sqs.at[1], sqp)
     total = jnp.sum(jnp.sum(total, axis=1, keepdims=True), axis=0, keepdims=True)
     factor_ref[...] = jnp.broadcast_to(lax.rsqrt(total / 16777216.0 + 1e-12), (8, 128))
     for quarter in range(4):
@@ -595,13 +647,13 @@
         for copy in o_copies(quarter):
             copy.wait_send()
 
-    @pl.when(s0 == 1)
+    @pl.when(sec < 4)
     def _():
         for c in range(1, NX):
             ring_sent(wide_ring(c))
             c_copy(c).wait_send()
 
-    for copy in qz + qx + qr:
+    for copy in qz + qp:
         copy.wait_send()
 
     def finish(m, carry):
@@ -611,7 +663,7 @@
             for copy in cot_copies(m, k):
                 copy.wait_send()
 
-        @pl.when(s0 == 0)
+        @pl.when(sec == 4)
         def _():
             for copy in act_copies(m, 1) + [relay_copy(m, 1)] + cot_copies(m, 2):
                 copy.wait_send()
@@ -670,7 +722,7 @@
             vmem((SEQ, D), BF16),
             vmem((SEQ, D), BF16),
             vmem((8, 3 * D), F32),
-            vmem((2, 16, SEQ), F32),
+            vmem((2, 4, SEQ), BF16),
             vmem((28, 128, OB), BF16),
             vmem((28, 128, OB), BF16),
             vmem((28, 128, OB), BF16),
@@ -678,25 +730,25 @@
             vmem((NX, 128, OB), F32),
             vmem((NX, 128, OB), BF16),
             vmem((NX - 1, 128, OB), BF16),
+            vmem((7, 8, NZ, 16, OB), F32),
             vmem((4, 2, NX * 16, OB), F32),
             vmem((4, NX * 16, OB), BF16),
             vmem((4, NX * 16, OB), BF16),
             vmem((3, NX, 16, OB), F32),
             vmem((NX, 16, OB), F32),
-            vmem((3, 8, 128), F32),
+            vmem((2, 8, 128), F32),
             vmem((NZ - 1, 8, 128), F32),
-            vmem((NX - 1, 8, 128), F32),
-            vmem((7, 8, 128), F32),
+            vmem((31, 8, 128), F32),
             dma((2, 2)), dma((2, 2)), dma((2,)), dma((2,)), dma((2,)), dma((2,)),
             dma((2, NX - 1, 6)), dma((2, NX - 1, 6)),
             dma((28,)), dma((28,)), dma((28,)), dma((28,)), dma((NX - 1,)), dma((NX - 1,)),
             dma((4,)), dma((4,)),
             dma((4, NX - 1)), dma((4, NX - 1)),
-            dma((NZ - 1,)), dma((NZ - 1,)), dma((NX - 1,)), dma((NX - 1,)), dma((7,)), dma((7,)),
+            dma((NZ - 1,)), dma((NZ - 1,)), dma((31,)), dma((31,)),
             dma((2,)),
         ],
         compiler_params=pltpu.CompilerParams(
-            collective_id=0, has_side_effects=True, vmem_limit_bytes=58 * 2**20
+            collective_id=0, has_side_effects=True, vmem_limit_bytes=62 * 2**20
         ),
         name="step",
     )(h0, mod, noise, w_qkv, w_out, head)
@@ -747,9 +799,7 @@
     h0 = jax.vmap(embed_sample, in_axes=(0, 0, 0, 0, None, None))(
         latents, noise, timesteps, cameras, embed_in, camera_table
     )
-    noise_rows = jnp.pad(noise.astype(F32), ((0, 0), (0, 12), (0, 0)))
-    head = jnp.pad(head_out, ((0, 12), (0, 0)))
-    qkv_rows, out_rows, factors = run_step(h0, mod, noise_rows, w_qkv[0], w_out[0], head)
+    qkv_rows, out_rows, factors = run_step(h0, mod, noise, w_qkv[0], w_out[0], head_out)
     return optimizer(
         qkv_rows, out_rows, factors, moment_qkv, moment_out, second_qkv, second_out
     )

time: 137 us -> 125 us (0.912)
  Pallas kernels: 129 us -> 117 us
    pallas_call x1, Pallas kernels: 126 us -> 114 us  [run_step(): pl.pallas_call(step_kernel, out_shape=(shape((16, 3 * D), F32), shape((16...]
where the time goes in v4:
time: 125 us; the launch traced here: 122 us
  Pallas kernels  117 us (94%)
  matrix products  3.96 us (3%)
    pallas_call x1, Pallas kernels, run_step(): pl.pallas_call(step_kernel, out_shape=(shape((16, 3 * D), F32), shape((16...  114 us

profile of v4, /device:TPU:8, one launch (start us, length us, event | category | flops | bytes accessed | tf_op | source)
XLA Modules:
  0.0 122.3 jit_solution(17787503896861208914)
XLA Ops:
  0.6 0.0 copy-start
  0.6 0.0 copy-start.1
  0.7 0.8 fusion.12
  1.5 1.1 fusion.3
  2.5 0.1 add.25
  2.7 1.9 %fusion.2.h0_ref = bf16[2,128,1024]{2,1,0:T(8,128)(2,1)} fusion(f32[2,128,1024]{2,1,0:T(8,128)S(1)} %bitcast.13, bf16[4,1024]{1,0:T(4,128)(2,1)} %param.18, bf16[2,4,128]{2,1,0:T(4,128)(2,1)} %noise_ref.1, bf16[2,4,128]{2,1,0:T(4,128)(2,1)} %param.14, f32[2]{0:T(128)S(1)} %get-tuple-element.15, f32[2]{0:T(128)S(1)} %get-tuple-element.14), kind=kOutput, calls=%fused_computation.3 | convolution fusion | flops 2627584 | bytes 1585168 | tf_op jit(solution)/shard_map/vmap()/dot_general | solution.py:43
  4.6 0.0 copy-done.1
  4.6 0.1 multiply_cosine_fusion
  4.8 0.0 copy-done
  4.8 1.0 fusion.mod_ref
  5.7 114.4 %step.1 = (f32[16,3072]{1,0:T(8,128)}, f32[16,1024]{1,0:T(8,128)}, f32[8,128]{1,0:T(8,128)}) custom-call(bf16[2,128,1024]{2,1,0:T(8,128)(2,1)} %fusion.2.h0_ref, f32[8,3072]{1,0:T(8,128)} %fusion.mod_ref, bf16[2,4,128]{2,1,0:T(4,128)(2,1)} %noise_ref.1, bf16[1024,3072]{1,0:T(8,128)(2,1)} %bitcast.12, bf16[1024,1024]{1,0:T(8,128)(2,1)} %bitcast.14, ...), custom_call_target="tpu_custom_call" | custom-call | tf_op jit(solution)/shard_map/step/pallas_call | solution.py:695
  120.2 2.1 %optimizer.1 = (f32[1,16,3072]{2,1,0:T(8,128)}, f32[1,16,1024]{2,1,0:T(8,128)}, f32[1,16,3072]{2,1,0:T(8,128)}, f32[1,16,1024]{2,1,0:T(8,128)}, f32[1,16,3072]{2,1,0:T(8,128)}, /*index=5*/f32[1,16,1024]{2,1,0:T(8,128)}) custom-call(f32[16,3072]{1,0:T(8,128)} %get-tuple-element.9.gq, f32[16,1024]{1,0:T(8,128)} %get-tuple-element.10.go, ...), custom_call_target="tpu_custom_call" | custom-call | tf_op jit(solution)/shard_map/optimizer/pallas_call | solution.py:771
  (3 shorter events, 0.0 us)
Async XLA Ops:
  0.6 4.1 %copy-start = (bf16[1,256,3072]{2,1,0:T(8,128)(2,1)S(1)}, bf16[1,256,3072]{2,1,0:T(8,128)(2,1)}, u32[]{:S(2)}) copy-start(bf16[1,256,3072]{2,1,0:T(8,128)(2,1)} %param.20) | copy-start | bytes 4718596
  0.6 4.0 %copy-start.1 = (s32[2]{0:T(128)S(1)}, s32[2]{0:T(128)}, u32[]{:S(2)}) copy-start(s32[2]{0:T(128)} %param.16) | copy-start | bytes 28
